TPU v7x, 8 devices: a whole 2x2x1 slice. The times are simulated.
8 devices in a mesh: data: 2 (over z, y), seq: 4 (over x, core).
Axes of the slice: x: 2, y: 2, z: 1, core: 2. Of those that a mesh axis runs over, the one named last changes fastest.
Arguments:
- x: bfloat16 [32768, 2048], P(('data', 'seq')), parts along dimension 0
- dout: bfloat16 [32768, 2048], P(('data', 'seq')), parts along dimension 0
- W_in: bfloat16 [2048, 8512], replicated
- conv_w: float32 [4, 4352], replicated
- conv_b: float32 [4352], replicated
- dt_bias: float32 [64], replicated
- A_log: float32 [64], replicated
- D_skip: float32 [64], replicated
- norm_w: float32 [4096], replicated
- W_out: bfloat16 [4096, 2048], replicated
Outputs:
- output 1: bfloat16 [32768, 2048], P(('data', 'seq')), parts along dimension 0
- output 2: bfloat16 [4096, 8512], P('data'), parts along dimension 0
- output 3: float32 [8, 4352], P('data'), parts along dimension 0
- output 4: float32 [8704], P('data'), parts along dimension 0
- output 5: float32 [128], P('data'), parts along dimension 0
- output 6: float32 [128], P('data'), parts along dimension 0
- output 7: float32 [128], P('data'), parts along dimension 0
- output 8: float32 [8192], P('data'), parts along dimension 0
- output 9: bfloat16 [8192, 2048], P('data'), parts along dimension 0
There are 2 independent parts. A program takes and returns all parts, laid end to end along the dimension named above; an argument that names none is the same for every part.
All inputs are finite; a program needn't handle non-finite values.
Results may differ from a plain program's by a relative error of at most 0.00793302.
Values are sent between devices in bfloat16 or wider.
A program may use at most 1 GiB of HBM per device.

v0:
```python
import functools
import jax
import jax.numpy as jnp
from jax import lax
from jax.sharding import PartitionSpec as P

CHUNK = 256
DSTATE = 128
KCONV = 4
EPS = 1e-5
F32 = jnp.float32
BF16 = jnp.bfloat16
HI = lax.Precision.HIGHEST


def _silu(v):
    return v * jax.nn.sigmoid(v)


def _prefix(s):
    k = s.shape[0]
    cs = jnp.cumsum(s, 0)
    diff = (cs - s)[:, None] - cs[None, :]
    m = (jnp.arange(k)[:, None] > jnp.arange(k)[None, :]).reshape((k, k) + (1,) * (s.ndim - 1))
    return jnp.where(m, jnp.exp(jnp.where(m, diff, 0.0)), 0.0)


def _mix(w, h):
    return jnp.sum(w[..., None, None] * h, 0)


def _tn(a, b):
    return lax.dot_general(a, b, (((0,), (0,)), ((), ())), preferred_element_type=F32)


def _nt(a, b):
    return lax.dot_general(a, b, (((1,), (1,)), ((), ())), preferred_element_type=F32)


def _pre(ext, dtr, conv_w, conv_b, dt_bias, A_log):
    t = dtr.shape[0]
    u = conv_b + sum(conv_w[j] * ext[KCONV - 1 - j:KCONV - 1 - j + t] for j in range(KCONV))
    dt = jax.nn.softplus(dtr + dt_bias)
    return _silu(u).astype(BF16), dt, -jnp.exp(A_log) * dt


def _blocks(xc, dt, a, G):
    t, H = dt.shape
    E = xc.shape[1] - 2 * G * DSTATE
    nc = t // CHUNK
    X = xc[:, :E].reshape(nc, CHUNK, G, H // G, E // H)
    B = xc[:, E:E + G * DSTATE].reshape(nc, CHUNK, G, DSTATE)
    C = xc[:, E + G * DSTATE:].reshape(nc, CHUNK, G, DSTATE)
    r = jnp.arange(CHUNK)
    tri = (r[:, None] >= r[None, :]).astype(F32)
    acs = jnp.einsum('qs,csh->cqh', tri, a.reshape(nc, CHUNK, H), precision=HI)
    return X, B, C, dt.reshape(nc, CHUNK, G, H // G), acs.reshape(nc, CHUNK, G, H // G)


def _states(xc, dt, a, G):
    X, B, _, dtc, acs = _blocks(xc, dt, a, G)
    ae = acs[:, -1]
    xw = (X * (dtc * jnp.exp(ae[:, None] - acs))[..., None]).astype(BF16)
    st = lax.dot_general(xw, B, (((1,), (1,)), ((0, 2), (0, 2))), preferred_element_type=F32)
    hst = jnp.sum(_prefix(ae)[..., None, None] * st[None], 1)
    s = jnp.sum(ae, 0)
    h_loc = _mix(jnp.exp(s - jnp.cumsum(ae, 0)), st)
    return hst, s, h_loc


def _inter(C, acs, ce, hst, h_in):
    hs = (hst + jnp.exp(ce)[..., None, None] * h_in).astype(BF16)
    return jnp.exp(acs)[..., None] * jnp.einsum('cqgn,cgkpn->cqgkp', C, hs, preferred_element_type=F32)


def _ssd(xc, dt, a, hst, h_in, G):
    X, B, C, dtc, acs = _blocks(xc, dt, a, G)
    ae = acs[:, -1]
    ce = jnp.cumsum(ae, 0) - ae
    q = acs.shape[1]
    m = jnp.tril(jnp.ones((q, q), bool))
    at = jnp.moveaxis(acs, 1, -1)
    seg = jnp.where(m, at[..., :, None] - at[..., None, :], 0.0)
    w = jnp.where(m, jnp.exp(seg) * jnp.moveaxis(dtc, 1, -1)[..., None, :], 0.0)
    cb = jnp.einsum('cqgn,csgn->cgqs', C, B, preferred_element_type=F32)
    sc = (cb[:, :, None] * w).astype(BF16)
    y = jnp.einsum('cgkqs,csgkp->cqgkp', sc, X, preferred_element_type=F32)
    y = y + _inter(C, acs, ce, hst, h_in)
    return y.reshape(xc.shape[0], -1)


def _gate(y1, xc, zf, D_skip, norm_w, G):
    t, E = y1.shape
    H = D_skip.shape[0]
    y = y1.reshape(t, H, E // H) + D_skip[:, None] * xc[:, :E].reshape(t, H, E // H)
    y = y.reshape(t, E) * _silu(zf)
    yg = y.reshape(t, G, E // G)
    yg = yg * lax.rsqrt(jnp.mean(yg * yg, -1, keepdims=True) + EPS)
    return (yg.reshape(t, E) * norm_w).astype(BF16)


def _out(xc, dt, a, hst, h_in, zf, D_skip, norm_w, G):
    return _gate(_ssd(xc, dt, a, hst, h_in, G), xc, zf, D_skip, norm_w, G)


def solution(mesh):
    nseq = mesh.shape['seq']
    fwd = [(i, i + 1) for i in range(nseq - 1)]
    bwd = [(i + 1, i) for i in range(nseq - 1)]

    def local(x, dout, W_in, conv_w, conv_b, dt_bias, A_log, D_skip, norm_w, W_out):
        t = x.shape[0]
        E = norm_w.shape[0]
        CD = conv_w.shape[1]
        G = (CD - E) // (2 * DSTATE)
        idx = lax.axis_index('seq')
        zx = jnp.dot(x, W_in, preferred_element_type=F32).astype(BF16)
        zf = zx[:, :E].astype(F32)
        xbc = zx[:, E:E + CD]
        halo = lax.ppermute(xbc[t - KCONV + 1:], 'seq', fwd)
        ext = jnp.concatenate([halo, xbc], 0).astype(F32)
        (xc, dt, a), pre_vjp = jax.vjp(_pre, ext, zx[:, E + CD:].astype(F32), conv_w, conv_b, dt_bias, A_log)
        (hst, s, h_loc), st_vjp = jax.vjp(functools.partial(_states, G=G), xc, dt, a)
        s_all = lax.all_gather(s, 'seq')
        h_all = lax.all_gather(h_loc, 'seq')
        wd = _prefix(s_all)
        h_in = _mix(wd[idx], h_all)
        yn, out_vjp = jax.vjp(functools.partial(_out, G=G), xc, dt, a, hst, h_in, zf, D_skip, norm_w)
        dyn = _nt(dout, W_out).astype(BF16)
        dW_out = _tn(yn, dout)
        dxc1, ddt1, da1, dhst, g_loc, dzf, dD, dnw = out_vjp(dyn)
        g_all = lax.all_gather(g_loc, 'seq')
        dh_fin = _mix(wd[:, idx], g_all)
        ds = jnp.sum(dh_fin * h_in, (-2, -1)) * jnp.exp(s)
        dxc2, ddt2, da2 = st_vjp((dhst, ds, dh_fin))
        dext, ddtr, dcw, dcb, ddtb, dal = pre_vjp((dxc1 + dxc2, ddt1 + ddt2, da1 + da2))
        dhalo = lax.ppermute(dext[:KCONV - 1], 'seq', bwd)
        dxbc = jnp.concatenate([dext[KCONV - 1:t], dext[t:] + dhalo], 0)
        dzx = jnp.concatenate([dzf, dxbc, ddtr], 1).astype(BF16)
        dx = _nt(dzx, W_in).astype(BF16)
        dW_in = _tn(x, dzx)
        dW_in, dcw, dcb, ddtb, dal, dD, dnw, dW_out = lax.psum((dW_in, dcw, dcb, ddtb, dal, dD, dnw, dW_out), 'seq')
        return dx, dW_in.astype(BF16), dcw, dcb, ddtb, dal, dD, dnw, dW_out.astype(BF16)

    xs = P(('data', 'seq'), None)
    return jax.shard_map(local, mesh=mesh, in_specs=(xs, xs) + (P(),) * 8,
                         out_specs=(xs, P('data', None), P('data', None), P('data'), P('data'), P('data'),
                                    P('data'), P('data'), P('data', None)),
                         check_vma=False)
```

profile of v0, /device:TPU:0, one launch (start us, length us, event | category | flops | bytes accessed | tf_op | source)
XLA Modules:
  0.0 5533.3 jit_solution(7681556629638943674)
XLA Ops:
  7.3 160.6 %convolution_convert_fusion.1 = bf16[4096,8512]{1,0:T(8,128)(2,1)} fusion(bf16[4096,2048]{1,0:T(8,128)(2,1)} %param.10, bf16[2048,8512]{0,1:T(8,128)(2,1)} %param.12), kind=kOutput, calls=%fused_computation.46 | convolution fusion | flops 142842527744 | bytes 121372672 | tf_op jit(solution)/shard_map/dot_general | solution.py:117
  168.7 2.9 collective-permute-start
  171.7 3.8 broadcast_multiply_fusion.4
  180.1 5.0 bitcast_exponential_fusion
  185.3 24.4 slice.83
  209.8 3.9 copy.322
  213.7 34.4 maximum_convert_fusion
  248.1 124.6 %multiply_convert_fusion.3 = (bf16[4096,4352]{1,0:T(8,128)(2,1)}, f32[4096,4352]{1,0:T(8,128)}) fusion(f32[4099,4352]{1,0:T(8,128)} %maximum_convert_fusion, f32[4352]{0:T(1024)S(1)} %get-tuple-element.28, f32[4352]{0:T(1024)S(1)} %get-tuple-element.29, f32[4352]{0:T(1024)S(1)} %get-tuple-element.27, f32[4352]{0:T(1024)S(1)} %get-tuple-element.26, ...), kind=kLoop, calls=%fused_computation.40 | loop fusion | flops 231735296 | bytes 392254464 | tf_op jit(solution)/shard_map/jvp()/convert_element_type | solution.py:44
  372.7 2.7 fusion.114
  375.4 42.1 slice_convert_fusion.1
  417.5 41.0 copy.312
  458.5 23.2 copy.382
  481.7 23.0 multiply_convert_fusion.6
  504.7 30.9 multiply_reduce_fusion.12
  535.7 3.5 copy.336
  543.1 9.2 all-reduce.16
  552.3 3.5 copy.317
  558.0 104.0 %reshape.831 = f32[16,256,1,64,64]{4,3,1,0,2:T(8,128)} reshape(f32[4096,4096]{1,0:T(8,128)} %get-tuple-element.56) | data formatting | bytes 134217728 | tf_op jit(solution)/shard_map/jvp()/convert_element_type | solution.py:63
  662.0 103.0 %copy.341 = f32[16,256,1,64,64]{1,4,3,0,2:T(8,128)} copy(f32[16,256,1,64,64]{4,3,1,0,2:T(8,128)} %reshape.831) | data formatting | bytes 134217728 | tf_op jit(solution)/shard_map/jvp()/convert_element_type | solution.py:63
  765.0 2.7 fusion.120
  767.8 113.9 %multiply_reduce_fusion.2 = f32[16,64,64,128]{3,2,1,0:T(8,128)} fusion(f32[16,64,64,128]{3,2,1,0:T(8,128)} %get-tuple-element.73, f32[16,16,64]{2,1,0:T(8,128)S(1)} %fusion.97), kind=kLoop, calls=%fused_computation.2 | loop fusion | flops 260046848 | bytes 67174400 | tf_op jit(solution)/shard_map/jvp()/reduce_sum | solution.py:65
  881.7 4.2 multiply_reduce_fusion.14
  885.9 34.0 fusion.64
  919.9 140.9 %bitcast_add_fusion = f32[16,256,1,64,64]{1,4,3,0,2:T(8,128)} fusion(f32[16,64,64,256]{3,2,1,0:T(8,128)} %fusion.64, f32[16,256,64]{1,2,0:T(8,128)} %copy.317, f32[16,64,256]{2,1,0:T(8,128)} %copy.314, f32[16,64,256]{2,1,0:T(8,128)} %copy-done.21, f32[16,256,256]{2,1,0:T(8,128)} %fusion.120, pred[256,256]{1,0:T(8,128)(4,1)S(1)} %copy-done.58, ...), kind=kOutput, calls=%fused_computation.55 | convolution fusion | flops 9026142208 | bytes 175177728 | tf_op jit(solution)/shard_map/jvp(cgkqs,csgkp->cqgkp)/dot_general | solution.py:87
  1060.9 115.6 %copy.371 = f32[16,256,1,64,64]{4,3,1,0,2:T(8,128)} copy(f32[16,256,1,64,64]{1,4,3,0,2:T(8,128)} %bitcast_add_fusion) | data formatting | bytes 134217728 | tf_op jit(solution)/shard_map/jvp()/reshape;jvp()/reshape | solution.py:95
  1176.5 108.0 %reshape.828 = f32[4096,4096]{1,0:T(8,128)} reshape(f32[16,256,1,64,64]{4,3,1,0,2:T(8,128)} %copy.371) | data formatting | bytes 134217728 | tf_op jit(solution)/shard_map/jvp()/reshape;jvp()/reshape | solution.py:95
  1284.5 65.0 %multiply_reduce_fusion.8 = (f32[4096]{0:T(1024)S(1)}, f32[4096,4096]{1,0:T(8,128)}) fusion(bf16[4096,8512]{1,0:T(8,128)(2,1)} %convolution_convert_fusion.1, f32[4096,4096]{1,0:T(8,128)} %reshape.828, bf16[4096,4352]{1,0:T(8,128)(2,1)} %get-tuple-element.46, f32[4096]{0:T(1024)S(1)} %copy-done.32), kind=kLoop, calls=%fused_computation.71 | loop fusion | flops 184545280 | bytes 201359360 | tf_op jit(solution)/shard_map/jvp()/reduce_sum | solution.py:98
  1349.5 84.5 %fusion.36 = f32[4096,2048]{1,0:T(8,128)} fusion(bf16[4096,2048]{1,0:T(8,128)(2,1)} %param.11, f32[4096,4096]{1,0:T(8,128)} %get-tuple-element.45, f32[4096]{0:T(1024)S(1)} %fusion.101, f32[4096]{0:T(1024)S(1)} %copy-done.65), kind=kOutput, calls=%fused_computation.83 | convolution fusion | flops 68769808384 | bytes 117473280 | tf_op jit(solution)/shard_map/dot_general | solution.py:33
  1434.0 99.7 %fusion.18 = (f32[4096]{0:T(1024)}, f32[4096]{0:T(1024)S(1)}, bf16[4096,4096]{1,0:T(8,128)(2,1)}) fusion(f32[4096,4096]{1,0:T(8,128)} %get-tuple-element.45, f32[4096]{0:T(1024)S(1)} %fusion.101, f32[4096]{0:T(1024)S(1)} %copy-done.65, bf16[4096,2048]{1,0:T(8,128)(2,1)} %param.11, bf16[4096,2048]{1,0:T(8,128)(2,1)} %param.19), kind=kOutput, calls=%fused_computation.48 | convolution fusion | flops 68853694464 | bytes 134283264 | tf_op jit(solution)/shard_map/dot_general | solution.py:37
  1534.5 110.9 %multiply_reduce_fusion.7 = (f32[4096]{0:T(1024)}, f32[4096,4096]{1,0:T(8,128)}, bf16[4096,4096]{1,0:T(8,128)(2,1)}) fusion(bf16[4096,4352]{1,0:T(8,128)(2,1)} %get-tuple-element.46, bf16[4096,8512]{1,0:T(8,128)(2,1)} %convolution_convert_fusion.1, f32[4096,4096]{1,0:T(8,128)} %get-tuple-element.45, f32[4096]{0:T(1024)S(1)} %multiply_multiply_fusion.1, ...), kind=kLoop, calls=%fused_computation.69 | loop fusion | flops 419426304 | bytes 335626240 | tf_op jit(solution)/shard_map/transpose(jvp())/reduce_sum | solution.py:95
  1645.4 65.8 %copy.326 = f32[4096,4096]{0,1:T(8,128)} copy(f32[4096,4096]{1,0:T(8,128)} %get-tuple-element.38) | data formatting | bytes 134217728 | tf_op jit(solution)/shard_map/transpose(jvp())/mul | solution.py:96
  1711.2 46.2 copy.383
  1757.4 264.2 %fusion.8 = (f32[16,64,256]{2,1,0:T(8,128)}, f32[16,64,256]{2,1,0:T(8,128)}, f32[16,64,256]{2,1,0:T(8,128)}, bf16[16,256,256]{2,1,0:T(8,128)(2,1)}) fusion(f32[16,64,256]{2,1,0:T(8,128)S(1)} %copy-done.27, f32[16,64,256]{2,1,0:T(8,128)S(1)} %copy-done.22, f32[16,256,256]{2,1,0:T(8,128)} %fusion.120, pred[256,256]{1,0:T(8,128)(4,1)S(1)} %copy-done.59, ...), kind=kOutput, calls=%fused_computation.16 | convolution fusion | flops 9661841408 | bytes 112263168 | tf_op jit(solution)/shard_map/transpose(jvp(cgkqs,csgkp->cqgkp))/dot_general | solution.py:87
  2021.6 96.9 %convert_bitcast_fusion.1 = bf16[16,256,1,64,64]{1,4,3,0,2:T(8,128)(2,1)} fusion(f32[16,64,256]{2,1,0:T(8,128)S(1)} %copy-done.27, f32[16,64,256]{2,1,0:T(8,128)S(1)} %copy-done.22, f32[16,256,256]{2,1,0:T(8,128)} %fusion.120, pred[256,256]{1,0:T(8,128)(4,1)S(1)} %copy-done.59, f32[16,64,64,256]{3,0,2,1:T(8,128)} %bitcast.35), kind=kOutput, calls=%fused_computation.88 | convolution fusion | flops 8992587776 | bytes 107020288 | tf_op jit(solution)/shard_map/transpose(jvp(cgkqs,csgkp->cqgkp))/dot_general | solution.py:87
  2118.6 52.2 fusion.25
  2170.8 63.5 %fusion.115 = (f32[16,64,64,128]{3,2,1,0:T(8,128)}, bf16[16,64,64,128]{3,2,1,0:T(8,128)(2,1)}) fusion(bf16[16,256,128,1]{2,1,3,0:T(8,128)(2,1)S(1)} %bitcast.272, f32[16,256,1,64,64]{1,0,4,3,2:T(8,128)} %bitcast.109, f32[16,256,64]{1,2,0:T(8,128)S(1)} %copy-done.15), kind=kOutput, calls=%fused_computation.205 | convolution fusion | flops 4328521728 | bytes 119537664 | tf_op jit(solution)/shard_map/transpose(jvp(cqgn,cgkpn->cqgkp))/dot_general | solution.py:73
  2235.0 3.7 copy.347
  2238.8 3.3 fusion.121
  2242.1 2.6 copy.346
  2244.7 3.7 copy.348
  2248.4 3.2 copy.339
  2251.6 90.0 %copy.372 = bf16[16,256,1,64,64]{4,3,1,0,2:T(8,128)(2,1)} copy(bf16[16,256,1,64,64]{1,4,3,0,2:T(8,128)(2,1)} %convert_bitcast_fusion.1) | data formatting | bytes 67108864 | tf_op jit(solution)/shard_map/transpose(jvp())/reshape | solution.py:51
  2341.6 86.7 %reshape.829 = bf16[4096,4096]{1,0:T(8,128)(2,1)} reshape(bf16[16,256,1,64,64]{4,3,1,0,2:T(8,128)(2,1)} %copy.372) | data formatting | bytes 67108864 | tf_op jit(solution)/shard_map/transpose(jvp())/reshape | solution.py:51
  2428.3 166.4 %multiply_reduce_fusion = (f32[16,16,64]{2,1,0:T(8,128)S(1)}, f32[16,64,64,128]{3,2,1,0:T(8,128)}) fusion(f32[16,64,64,128]{3,2,1,0:T(8,128)} %get-tuple-element.75, f32[16,64,64,128]{3,2,1,0:T(8,128)} %get-tuple-element.73, f32[16,16,64]{2,1,0:T(8,128)S(1)} %copy-done.26), kind=kLoop, calls=%fused_computation | loop fusion | flops 528465920 | bytes 100794368 | tf_op jit(solution)/shard_map/transpose(jvp())/reduce_sum | solution.py:65
  2595.5 15.6 multiply_reduce_fusion.10
  2611.2 65.4 %bitcast_convert_fusion.1 = bf16[16,256,128]{2,1,0:T(8,128)(2,1)} fusion(f32[16,64,64,128]{3,2,1,0:T(8,128)} %multiply_reduce_fusion.2, f32[64,64,128]{2,1,0:T(8,128)S(1)} %copy-done.1, f32[16,64]{1,0:T(8,128)S(1)} %copy-done.24, f32[16,256,1,64,64]{1,0,4,3,2:T(8,128)} %bitcast.109, f32[16,256,64]{1,2,0:T(8,128)} %copy.317), kind=kOutput, calls=%fused_computation.132 | convolution fusion | flops 4337434624 | bytes 104861696 | tf_op jit(solution)/shard_map/transpose(jvp(cqgn,cgkpn->cqgkp))/dot_general | solution.py:73
  2676.6 3.6 fusion.83
  2680.2 32.9 multiply_convert_fusion.5
  2713.2 4.3 multiply_reduce_fusion.13
  2717.5 15.3 multiply_reduce_fusion.9
  2733.9 42.0 fusion.90
  2778.2 47.1 fusion.29
  2825.3 90.0 %copy.373 = bf16[16,256,1,64,64]{4,3,1,0,2:T(8,128)(2,1)} copy(bf16[16,256,1,64,64]{1,4,3,0,2:T(8,128)(2,1)} %get-tuple-element.61) | data formatting | bytes 67108864 | tf_op jit(solution)/shard_map/transpose(jvp())/reshape | solution.py:51
  2915.3 86.8 %reshape.830 = bf16[4096,4096]{1,0:T(8,128)(2,1)} reshape(bf16[16,256,1,64,64]{4,3,1,0,2:T(8,128)(2,1)} %copy.373) | data formatting | bytes 67108864 | tf_op jit(solution)/shard_map/transpose(jvp())/reshape | solution.py:51
  3002.2 164.3 %multiply_reduce_fusion.6 = (f32[4352]{0:T(1024)}, f32[4352]{0:T(1024)}, f32[4352]{0:T(1024)}, f32[4352]{0:T(1024)}, f32[4352]{0:T(1024)}, /*index=5*/f32[4096,4352]{1,0:T(8,128)}) fusion(f32[4099,4352]{1,0:T(8,128)} %maximum_convert_fusion, f32[4096,4352]{1,0:T(8,128)} %get-tuple-element.47, bf16[4096,4096]{1,0:T(8,128)(2,1)} %reshape.830, ...), kind=kLoop, calls=%fused_computation.39 | loop fusion | flops 534752000 | bytes 531715072 | tf_op jit(solution)/shard_map/transpose(jvp())/reduce_sum | solution.py:42
  3166.4 113.2 %broadcast_multiply_fusion = (f32[4096,4352]{1,0:T(8,128)}, f32[4096,4352]{1,0:T(8,128)}, f32[4096,4352]{1,0:T(8,128)}, f32[4096,4352]{1,0:T(8,128)}) fusion(f32[4096,4352]{1,0:T(8,128)} %get-tuple-element.41, f32[4352]{0:T(1024)S(1)} %copy-done.40, f32[4352]{0:T(1024)S(1)} %copy-done.36, f32[4352]{0:T(1024)S(1)} %copy-done.38, f32[4352]{0:T(1024)S(1)} %copy-done.42), kind=kLoop, calls=%fused_computation.79 | loop fusion | flops 71303168 | bytes 356585472 | tf_op jit(solution)/shard_map/transpose(jvp())/mul | solution.py:42
  3280.9 98.8 %pad_add_fusion = bf16[4099,4352]{1,0:T(8,128)(2,1)} fusion(f32[4096,4352]{1,0:T(8,128)} %get-tuple-element.51, f32[4096,4352]{1,0:T(8,128)} %get-tuple-element.52, f32[4096,4352]{1,0:T(8,128)} %get-tuple-element.53, f32[4096,4352]{1,0:T(8,128)} %get-tuple-element.50), kind=kLoop, calls=%fused_computation.32 | loop fusion | flops 71355392 | bytes 320890368 | tf_op jit(solution)/shard_map/transpose(jvp())/add_any | solution.py:42
  3382.4 5.0 fusion.112
  3389.7 3.4 fusion.69
  3399.7 4.9 fusion.109
  3405.8 24.8 slice.131
  3431.7 173.6 %convolution_bitcast_fusion = f32[2048,8512]{0,1:T(8,128)} fusion(bf16[4096,2048]{1,0:T(8,128)(2,1)} %param.10, bf16[3,4352]{1,0:T(4,128)(2,1)S(1)} %fusion.100, bf16[4093,4352]{1,0:T(8,128)(2,1)} %slice.131, bf16[4096,64]{1,0:T(8,128)(2,1)S(1)} %get-tuple-element.40, bf16[4096,4096]{1,0:T(8,128)(2,1)} %get-tuple-element.48), kind=kOutput, calls=%fused_computation.77 | convolution fusion | flops 143086583808 | bytes 156237824 | tf_op jit(solution)/shard_map/dot_general | solution.py:33
  3605.3 1734.8 %all-reduce.22 = (bf16[2048,8512]{0,1:T(8,128)(2,1)}, f32[4352]{0:T(1024)}, f32[64]{0:T(128)}, f32[64]{0:T(128)}, f32[64]{0:T(128)}, /*index=5*/f32[4096]{0:T(1024)}, bf16[4096,2048]{1,0:T(8,128)(2,1)}) all-reduce(f32[2048,8512]{0,1:T(8,128)} %convolution_bitcast_fusion, ...), channel_id=1, replica_groups=mesh['data'=2,'seq'=4] {'seq'}, use_global_device_ids=true, to_apply=%region_28.29 | all-reduce | flops 25829824 | bytes 154996224 | tf_op jit(solution)/shard_map/psum | solution.py:142
  5340.1 184.7 %convolution_convert_fusion.3 = bf16[4096,2048]{1,0:T(8,128)(2,1)} fusion(bf16[2048,8512]{0,1:T(8,128)(2,1)} %param.12, bf16[3,4352]{1,0:T(4,128)(2,1)S(1)} %fusion.100, bf16[4093,4352]{1,0:T(8,128)(2,1)} %slice.131, bf16[4096,64]{1,0:T(8,128)(2,1)S(1)} %get-tuple-element.40, bf16[4096,4096]{1,0:T(8,128)(2,1)} %get-tuple-element.48), kind=kOutput, calls=%fused_computation.110 | convolution fusion | flops 143094972416 | bytes 121372672 | tf_op jit(solution)/shard_map/dot_general | solution.py:37
  (234 shorter events, 33.3 us)
Async XLA Ops:
  7.2 874.5 %all-gather.6.cloned.1.call-start = ((), (), s32[]{:S(2)}) async-start(), calls=%async_computation.1 | async-start | bytes 10485760 | tf_op jit(solution)/shard_map/all_gather | solution.py:125
  7.2 164.5 %copy-start.80 = (f32[64]{0:T(128)S(1)}, f32[64]{0:T(128)}, u32[]{:S(2)}) copy-start(f32[64]{0:T(128)} %param.16) | copy-start | bytes 772
  7.2 164.5 %copy-start.71 = (f32[64]{0:T(128)S(1)}, f32[64]{0:T(128)}, u32[]{:S(2)}) copy-start(f32[64]{0:T(128)} %param.15) | copy-start | bytes 772
  7.2 177.9 %copy-start.56 = (f32[4,4352]{1,0:T(4,128)S(1)}, f32[4,4352]{1,0:T(4,128)}, u32[]{:S(2)}) copy-start(f32[4,4352]{1,0:T(4,128)} %param.13) | copy-start | bytes 208900
  168.7 44.9 collective-permute-start
  185.3 62.8 %copy-start.35 = (f32[4352]{0:T(1024)}, f32[4352]{0:T(1024)S(1)}, u32[]{:S(2)}) copy-start(f32[4352]{0:T(1024)S(1)} %get-tuple-element.26) | copy-start | bytes 52228
  185.3 62.7 %copy-start.37 = (f32[4352]{0:T(1024)}, f32[4352]{0:T(1024)S(1)}, u32[]{:S(2)}) copy-start(f32[4352]{0:T(1024)S(1)} %get-tuple-element.27) | copy-start | bytes 52228
  185.3 62.7 %copy-start.39 = (f32[4352]{0:T(1024)}, f32[4352]{0:T(1024)S(1)}, u32[]{:S(2)}) copy-start(f32[4352]{0:T(1024)S(1)} %get-tuple-element.28) | copy-start | bytes 52228
  185.3 62.7 %copy-start.41 = (f32[4352]{0:T(1024)}, f32[4352]{0:T(1024)S(1)}, u32[]{:S(2)}) copy-start(f32[4352]{0:T(1024)S(1)} %get-tuple-element.29) | copy-start | bytes 52228
  375.4 389.6 %copy-start.6 = (bf16[4096,128]{1,0:T(8,128)(2,1)}, bf16[4096,128]{1,0:T(8,128)(2,1)S(1)}, u32[]{:S(2)}) copy-start(bf16[4096,128]{1,0:T(8,128)(2,1)S(1)} %get-tuple-element.59) | copy-start | bytes 3145732
  504.7 36.9 copy-start.82
  504.7 38.1 copy-start.68
  504.7 52.5 copy-start.29
  535.6 2177.6 %all-gather.8.cloned.1.call-start = ((), (), s32[]{:S(2)}) async-start(), calls=%async_computation.2 | async-start | bytes 10485760 | tf_op jit(solution)/shard_map/all_gather | solution.py:132
  555.8 106.2 %copy-start.63 = (pred[16,16]{1,0:T(8,128)(4,1)}, pred[16,16]{1,0:T(8,128)(4,1)S(1)}, u32[]{:S(2)}) copy-start(pred[16,16]{1,0:T(8,128)(4,1)S(1)} %iota_compare_fusion.4) | copy-start | bytes 772
  557.9 104.1 %copy-start.52 = (f32[16,64]{1,0:T(8,128)}, f32[16,64]{1,0:T(8,128)S(1)}, u32[]{:S(2)}) copy-start(f32[16,64]{1,0:T(8,128)S(1)} %fusion.103) | copy-start | bytes 12292
  558.0 209.8 %copy-start.25 = (f32[16,16,64]{2,1,0:T(8,128)}, f32[16,16,64]{2,1,0:T(8,128)S(1)}, u32[]{:S(2)}) copy-start(f32[16,16,64]{2,1,0:T(8,128)S(1)} %fusion.97) | copy-start | bytes 196612
  662.0 103.0 %copy-start.9 = (bf16[4096,128]{1,0:T(8,128)(2,1)S(1)}, bf16[4096,128]{1,0:T(8,128)(2,1)}, u32[]{:S(2)}) copy-start(bf16[4096,128]{1,0:T(8,128)(2,1)} %get-tuple-element.58) | copy-start | bytes 3145732
  767.8 118.1 %copy-start.10 = (bf16[4096,128]{1,0:T(8,128)(2,1)S(1)}, bf16[4096,128]{1,0:T(8,128)(2,1)}, u32[]{:S(2)}) copy-start(bf16[4096,128]{1,0:T(8,128)(2,1)} %get-tuple-element.58) | copy-start | bytes 3145732
  767.8 118.2 %copy-start.23 = (f32[16,64]{1,0:T(8,128)S(1)}, f32[16,64]{1,0:T(8,128)}, u32[]{:S(2)}) copy-start(f32[16,64]{1,0:T(8,128)} %get-tuple-element.70) | copy-start | bytes 12292
  1176.5 108.0 %copy-start.32 = (f32[4096]{0:T(1024)S(1)}, f32[4096]{0:T(1024)}, u32[]{:S(2)}) copy-start(f32[4096]{0:T(1024)} %mul.558) | copy-start | bytes 49156
  1284.5 65.0 %copy-start.65 = (f32[4096]{0:T(1024)S(1)}, f32[4096]{0:T(1024)}, u32[]{:S(2)}) copy-start(f32[4096]{0:T(1024)} %param.18) | copy-start | bytes 49156
  1349.5 84.5 %copy-start.43 = (f32[4096]{0:T(1024)}, f32[4096]{0:T(1024)S(1)}, u32[]{:S(2)}) copy-start(f32[4096]{0:T(1024)S(1)} %get-tuple-element.44) | copy-start | bytes 49156
  1434.0 100.5 %copy-start.33 = (f32[4096]{0:T(1024)S(1)}, f32[4096]{0:T(1024)}, u32[]{:S(2)}) copy-start(f32[4096]{0:T(1024)} %mul.558) | copy-start | bytes 49156
  1711.2 46.2 copy-start.22
  1711.2 46.2 copy-start.27
  1711.2 46.2 copy-start.59
  2118.6 52.2 copy-start.11
  2118.6 52.2 copy-start.15
  2170.8 63.5 %copy-start.57 = (f32[4096]{0:T(1024)S(1)}, f32[4096]{0:T(1024)}, u32[]{:S(2)}) copy-start(f32[4096]{0:T(1024)} %get-tuple-element.37) | copy-start | bytes 49156
  2341.6 86.7 %copy-start.26 = (f32[16,16,64]{2,1,0:T(8,128)S(1)}, f32[16,16,64]{2,1,0:T(8,128)}, u32[]{:S(2)}) copy-start(f32[16,16,64]{2,1,0:T(8,128)} %copy-done.25) | copy-start | bytes 196612
  2428.3 166.4 %copy-start.30 = (f32[16,1,64]{2,1,0:T(1,128)S(1)}, f32[16,1,64]{2,1,0:T(1,128)}, u32[]{:S(2)}) copy-start(f32[16,1,64]{2,1,0:T(1,128)} %copy-done.28) | copy-start | bytes 12292
  2428.3 166.4 %copy-start.53 = (f32[16,64]{1,0:T(8,128)S(1)}, f32[16,64]{1,0:T(8,128)}, u32[]{:S(2)}) copy-start(f32[16,64]{1,0:T(8,128)} %copy-done.52) | copy-start | bytes 12292
  2428.3 166.4 %copy-start.64 = (pred[16,16]{1,0:T(8,128)(4,1)S(1)}, pred[16,16]{1,0:T(8,128)(4,1)}, u32[]{:S(2)}) copy-start(pred[16,16]{1,0:T(8,128)(4,1)} %copy-done.63) | copy-start | bytes 772
  2428.3 167.2 %copy-start.1 = (f32[64,64,128]{2,1,0:T(8,128)S(1)}, f32[64,64,128]{2,1,0:T(8,128)}, u32[]{:S(2)}) copy-start(f32[64,64,128]{2,1,0:T(8,128)} %copy-done) | copy-start | bytes 6291460
  2428.3 167.2 %copy-start.24 = (f32[16,64]{1,0:T(8,128)S(1)}, f32[16,64]{1,0:T(8,128)}, u32[]{:S(2)}) copy-start(f32[16,64]{1,0:T(8,128)} %get-tuple-element.70) | copy-start | bytes 12292
  2611.1 65.5 %copy-start.7 = (bf16[4096,128]{1,0:T(8,128)(2,1)S(1)}, bf16[4096,128]{1,0:T(8,128)(2,1)}, u32[]{:S(2)}) copy-start(bf16[4096,128]{1,0:T(8,128)(2,1)} %copy-done.6) | copy-start | bytes 3145732
  2611.1 69.1 %copy-start.34 = (f32[4096]{0:T(1024)S(1)}, f32[4096]{0:T(1024)}, u32[]{:S(2)}) copy-start(f32[4096]{0:T(1024)} %mul.558) | copy-start | bytes 49156
  2611.2 2913.7 %all-reduce.21.cloned.1.call-start = ((), (), s32[]{:S(2)}) async-start(), calls=%async_computation | async-start | bytes 139264 | tf_op jit(solution)/shard_map/psum | solution.py:142
  2733.9 44.2 copy-start.8
  2915.3 86.8 %copy-start.17 = (bf16[16,256,128]{2,1,0:T(8,128)(2,1)S(1)}, bf16[16,256,128]{2,1,0:T(8,128)(2,1)}, u32[]{:S(2)}) copy-start(bf16[16,256,128]{2,1,0:T(8,128)(2,1)} %fusion.83) | copy-start | bytes 3145732
  2915.3 86.8 %copy-start.19 = (bf16[16,256,1,128]{3,1,0,2:T(8,128)(2,1)S(1)}, bf16[16,256,1,128]{3,1,0,2:T(8,128)(2,1)}, u32[]{:S(2)}) copy-start(bf16[16,256,1,128]{3,1,0,2:T(8,128)(2,1)} %copy.335) | copy-start | bytes 3145732
  2915.3 86.8 %copy-start.20 = (bf16[16,256,128]{2,1,0:T(8,128)(2,1)S(1)}, bf16[16,256,128]{2,1,0:T(8,128)(2,1)}, u32[]{:S(2)}) copy-start(bf16[16,256,128]{2,1,0:T(8,128)(2,1)} %fusion.121) | copy-start | bytes 3145732
  3002.1 164.3 %copy-start.36 = (f32[4352]{0:T(1024)S(1)}, f32[4352]{0:T(1024)}, u32[]{:S(2)}) copy-start(f32[4352]{0:T(1024)} %copy-done.35) | copy-start | bytes 52228
  3002.1 164.3 %copy-start.38 = (f32[4352]{0:T(1024)S(1)}, f32[4352]{0:T(1024)}, u32[]{:S(2)}) copy-start(f32[4352]{0:T(1024)} %copy-done.37) | copy-start | bytes 52228
  3002.1 164.3 %copy-start.40 = (f32[4352]{0:T(1024)S(1)}, f32[4352]{0:T(1024)}, u32[]{:S(2)}) copy-start(f32[4352]{0:T(1024)} %copy-done.39) | copy-start | bytes 52228
  3002.1 164.3 %copy-start.42 = (f32[4352]{0:T(1024)S(1)}, f32[4352]{0:T(1024)}, u32[]{:S(2)}) copy-start(f32[4352]{0:T(1024)} %copy-done.41) | copy-start | bytes 52228
  3280.7 98.9 %copy-start.14 = (f32[16,64]{1,0:T(8,128)S(1)}, f32[16,64]{1,0:T(8,128)}, u32[]{:S(2)}) copy-start(f32[16,64]{1,0:T(8,128)} %get-tuple-element.71) | copy-start | bytes 12292
  3280.8 98.9 %copy-start.51 = (f32[16,64]{1,0:T(8,128)S(1)}, f32[16,64]{1,0:T(8,128)}, u32[]{:S(2)}) copy-start(f32[16,64]{1,0:T(8,128)} %multiply_reduce_fusion.9) | copy-start | bytes 12292
  3280.8 99.0 %copy-start.4 = (f32[16,64,256]{1,0,2:T(8,128)S(1)}, f32[16,64,256]{1,0,2:T(8,128)}, u32[]{:S(2)}) copy-start(f32[16,64,256]{1,0,2:T(8,128)} %copy-done.3) | copy-start | bytes 3145732
  3280.8 99.0 %copy-start.31 = (f32[16,1,64]{2,1,0:T(1,128)S(1)}, f32[16,1,64]{2,1,0:T(1,128)}, u32[]{:S(2)}) copy-start(f32[16,1,64]{2,1,0:T(1,128)} %copy-done.28) | copy-start | bytes 12292
  3280.8 99.0 %copy-start.60 = (f32[16,64]{1,0:T(8,128)S(1)}, f32[16,64]{1,0:T(8,128)}, u32[]{:S(2)}) copy-start(f32[16,64]{1,0:T(8,128)} %get-tuple-element.22) | copy-start | bytes 12292
  3280.8 99.0 %copy-start.69 = (f32[64]{0:T(128)S(1)}, f32[64]{0:T(128)}, u32[]{:S(2)}) copy-start(f32[64]{0:T(128)} %copy-done.67) | copy-start | bytes 772
  3280.8 99.1 %copy-start.16 = (f32[16,256,64]{1,2,0:T(8,128)S(1)}, f32[16,256,64]{1,2,0:T(8,128)}, u32[]{:S(2)}) copy-start(f32[16,256,64]{1,2,0:T(8,128)} %get-tuple-element.60) | copy-start | bytes 3145732
  3280.8 101.6 %copy-start.50 = (f32[16,64]{1,0:T(8,128)S(1)}, f32[16,64]{1,0:T(8,128)}, u32[]{:S(2)}) copy-start(f32[16,64]{1,0:T(8,128)} %copy-done.49) | copy-start | bytes 12292
  3280.8 106.5 %copy-start.75 = (f32[64]{0:T(128)S(1)}, f32[64]{0:T(128)}, u32[]{:S(2)}) copy-start(f32[64]{0:T(128)} %multiply_reduce_fusion.15) | copy-start | bytes 772
  3280.8 106.5 %copy-start.55 = (f32[16,64]{1,0:T(8,128)S(1)}, f32[16,64]{1,0:T(8,128)}, u32[]{:S(2)}) copy-start(f32[16,64]{1,0:T(8,128)} %copy-done.54) | copy-start | bytes 12292
  3280.9 106.5 %copy-start.61 = (f32[16,1,1,64]{3,2,1,0:T(1,128)S(1)}, f32[16,1,1,64]{3,2,1,0:T(1,128)}, u32[]{:S(2)}) copy-start(f32[16,1,1,64]{3,2,1,0:T(1,128)} %fusion.119) | copy-start | bytes 12292
  3398.1 32.5 collective-permute-start.1
  3431.7 173.6 %copy-start.44 = (f32[4352]{0:T(1024)S(1)}, f32[4352]{0:T(1024)}, u32[]{:S(2)}) copy-start(f32[4352]{0:T(1024)} %get-tuple-element.19) | copy-start | bytes 52228
  3431.7 173.6 %copy-start.66 = (f32[4096]{0:T(1024)S(1)}, f32[4096]{0:T(1024)}, u32[]{:S(2)}) copy-start(f32[4096]{0:T(1024)} %get-tuple-element.17) | copy-start | bytes 49156
  3431.7 173.6 %copy-start.76 = (f32[64]{0:T(128)S(1)}, f32[64]{0:T(128)}, u32[]{:S(2)}) copy-start(f32[64]{0:T(128)} %reduce_sum.358) | copy-start | bytes 772
  3431.7 173.6 %copy-start.77 = (f32[64]{0:T(128)S(1)}, f32[64]{0:T(128)}, u32[]{:S(2)}) copy-start(f32[64]{0:T(128)} %get-tuple-element.39) | copy-start | bytes 772
  3431.7 173.6 %copy-start.79 = (f32[64]{0:T(128)S(1)}, f32[64]{0:T(128)}, u32[]{:S(2)}) copy-start(f32[64]{0:T(128)} %negate_multiply_fusion) | copy-start | bytes 772
  (24 other events, 517.7 us)
Sparse Core Ops, SparseCore 0:
  535.7 58.1 all-gather.5
  2611.3 56.7 all-gather.7
  3405.9 27.7 all-reduce.20
where the time goes:
time: 5560 us; the launch traced here: 5530 us
  blocking collectives  1740 us (31%)
  matrix products  1500 us (27%)
  other arithmetic  1210 us (22%)
  local copies, waits for them, and re-layouts  1050 us (19%)
    psum x1, blocking collectives, local(): lax.psum((dW_in, dcw, dcb, ddtb, dal, dD, dnw, dW_out), 'seq')  1730 us
    dot_general x3, matrix products, _ssd(): y = jnp.einsum('cgkqs,csgkp->cqgkp', sc, X, preferred_element_type=F32)  502 us
    reshape x4, local copies, waits for them, and re-layouts, _blocks(): X = xc[:, :E].reshape(nc, CHUNK, G, H // G, E // H)  353 us
    dot_general x2, matrix products, _nt(): lax.dot_general(a, b, (((1,), (1,)), ((), ())), preferred_element_type=F32)  284 us
    reduce_sum x2, other arithmetic, _states(): hst = jnp.sum(_prefix(ae)[..., None, None] * st[None], 1)  280 us
    dot_general x2, matrix products, _tn(): lax.dot_general(a, b, (((0,), (0,)), ((), ())), preferred_element_type=F32)  258 us
    reshape x2, local copies, waits for them, and re-layouts, _gate(): y1.reshape(t, H, E // H) + D_skip[:, None] * xc[:, :E].reshape(t, H, E // H)  224 us
    convert_element_type x2, local copies, waits for them, and re-layouts, _states(): xw = (X * (dtc * jnp.exp(ae[:, None] - acs))[..., None]).astype(BF16)  207 us
  transfers between devices with their start and end apart: 5, of which 0 were waited for; matrix products, arithmetic and copies ran while one was open for 16% of the time, Pallas kernels for 0%

commit v1 on v0

v1 whole, which is shorter than its diff:
```python
import jax
import jax.numpy as jnp
from jax import lax
from jax.experimental import pallas as pl
from jax.experimental.pallas import tpu as pltpu
from jax.sharding import PartitionSpec as P

Q = 256
N = 128
H = 64
E = 4096
CD = E + 2 * N
PX = CD + H
KCONV = 4
EPS = 1e-5
LOG2E = 1.4426950408889634
F32 = jnp.float32
BF16 = jnp.bfloat16
HI = lax.Precision.HIGHEST
HB = 128


def _dot(a, b):
    return lax.dot_general(a, b, (((1,), (0,)), ((), ())), preferred_element_type=F32)


def _tn(a, b):
    return lax.dot_general(a, b, (((0,), (0,)), ((), ())), preferred_element_type=F32)


def _nt(a, b):
    return lax.dot_general(a, b, (((1,), (1,)), ((), ())), preferred_element_type=F32)


def _lanes(j, w):
    return pl.ds(pl.multiple_of(j * w, w), w)


def _iota(shape, d):
    return lax.broadcasted_iota(jnp.int32, shape, d)


def _split3(v):
    hi = v.astype(BF16).astype(F32)
    mid = (v - hi).astype(BF16).astype(F32)
    lo = v - hi - mid
    return jnp.concatenate([hi, mid, lo, jnp.zeros_like(v)], 1).astype(BF16)


def _split2(v):
    hi = v.astype(BF16)
    return hi, (v - hi.astype(F32)).astype(BF16)


def _softplus(v):
    return jnp.maximum(v, 0.0) + jnp.log1p(jnp.exp(-jnp.abs(v)))


def _const(shape):
    return pl.BlockSpec(shape, lambda i: (0,) * len(shape), pipeline_mode=pl.Buffered(1))


def _params(mb, **kw):
    return pltpu.CompilerParams(dimension_semantics=('arbitrary',), vmem_limit_bytes=mb * 1024 * 1024, **kw)


def _cost(flops, nbytes):
    return pl.CostEstimate(flops=int(flops), bytes_accessed=int(nbytes), transcendentals=0)


def _taps(x_ref, halo_ref, r):
    cur = x_ref[pl.ds(pl.multiple_of(r * Q, Q), Q), :].astype(F32)
    at = pl.multiple_of(jnp.maximum(r * Q - 16, 0), 16)
    prev = jnp.where(r == 0, halo_ref[...], x_ref[pl.ds(at, 16), :]).astype(F32)
    ext = jnp.concatenate([prev, cur], 0)
    return [cur] + [pltpu.roll(ext, k, 0)[16:] for k in range(1, KCONV)]


def _conv_fwd_kernel(x_ref, halo_ref, w_ref, b_ref, o_ref):
    nr = x_ref.shape[0] // Q

    def body(r, _):
        taps = _taps(x_ref, halo_ref, r)
        u = b_ref[...] + sum(w_ref[k:k + 1, :] * taps[k] for k in range(KCONV))
        o_ref[pl.ds(pl.multiple_of(r * Q, Q), Q), :] = (u * jax.nn.sigmoid(u)).astype(BF16)
        return 0

    lax.fori_loop(0, nr, body, 0)


def _conv_fwd(xb, halo, w, b, cw=256):
    t = xb.shape[0]
    return pl.pallas_call(
        _conv_fwd_kernel,
        grid=(CD // cw,),
        in_specs=[pl.BlockSpec((t, cw), lambda i: (0, i)), pl.BlockSpec((16, cw), lambda i: (0, i)),
                  pl.BlockSpec((KCONV, cw), lambda i: (0, i)), pl.BlockSpec((1, cw), lambda i: (0, i))],
        out_specs=pl.BlockSpec((t, cw), lambda i: (0, i)),
        out_shape=jax.ShapeDtypeStruct((t, CD), BF16),
        compiler_params=_params(40),
        cost_estimate=_cost(25e9, 4 * t * CD),
        name='conv_fwd',
    )(xb, halo, w, b)


def _conv_bwd_kernel(x_ref, halo_ref, d_ref, w_ref, b_ref, o_ref, gw_ref, gb_ref, head_ref, tail_ref, nxt):
    nr = x_ref.shape[0] // Q
    cw = x_ref.shape[1]
    gw_ref[...] = jnp.zeros_like(gw_ref)
    gb_ref[...] = jnp.zeros_like(gb_ref)
    nxt[...] = jnp.zeros_like(nxt)

    def fold(v):
        return jnp.sum(v.reshape(Q // 8, 8, cw), 0)

    def body(k, _):
        r = nr - 1 - k
        taps = _taps(x_ref, halo_ref, r)
        u = b_ref[...] + sum(w_ref[i:i + 1, :] * taps[i] for i in range(KCONV))
        sg = jax.nn.sigmoid(u)
        rows = pl.ds(pl.multiple_of(r * Q, Q), Q)
        du = d_ref[rows, :].astype(F32) * (sg * (1.0 + u * (1.0 - sg)))
        gb_ref[...] += fold(du)
        for i in range(KCONV):
            gw_ref[8 * i:8 * i + 8, :] += fold(du * taps[i])
        ext = jnp.concatenate([du, nxt[...]], 0)
        dx = w_ref[0:1, :] * du + sum(
            w_ref[i:i + 1, :] * pltpu.roll(ext, Q + 8 - i, 0)[:Q] for i in range(1, KCONV))
        nxt[...] = du[:8]
        o_ref[rows, :] = dx.astype(BF16)

        @pl.when(k == 0)
        def _():
            tail_ref[...] = dx[Q - 16:]

        return 0

    lax.fori_loop(0, nr, body, 0)
    head_ref[...] = nxt[...]


def _conv_bwd(xb, halo, dxc, w, b, cw=256):
    t = xb.shape[0]
    col = lambda r: pl.BlockSpec((r, cw), lambda i: (0, i))
    return pl.pallas_call(
        _conv_bwd_kernel,
        grid=(CD // cw,),
        in_specs=[col(t), col(16), col(t), col(KCONV), col(1)],
        out_specs=[col(t), col(8 * KCONV), col(8), col(8), col(16)],
        out_shape=[jax.ShapeDtypeStruct((t, PX), BF16), jax.ShapeDtypeStruct((8 * KCONV, CD), F32),
                   jax.ShapeDtypeStruct((8, CD), F32), jax.ShapeDtypeStruct((8, CD), F32),
                   jax.ShapeDtypeStruct((16, CD), F32)],
        scratch_shapes=[pltpu.VMEM((8, cw), F32)],
        compiler_params=_params(40),
        cost_estimate=_cost(50e9, 6 * t * CD),
        name='conv_bwd',
    )(xb, halo, dxc, w, b)


def _state_kernel(xc_ref, dtr_ref, bias_ref, al_ref, e_ref, cd_ref, cdt_ref, hst_ref, h_ref, s_ref):
    i = pl.program_id(0)

    @pl.when(i == 0)
    def _():
        h_ref[...] = jnp.zeros_like(h_ref)
        s_ref[...] = jnp.zeros_like(s_ref)

    dt = _softplus(dtr_ref[...].astype(F32) + bias_ref[...])
    a = -jnp.exp(al_ref[...]) * dt
    tri = (_iota((Q, Q), 0) >= _iota((Q, Q), 1)).astype(F32)
    c = lax.dot_general(tri, a, (((1,), (0,)), ((), ())), precision=HI, preferred_element_type=F32)
    s_ref[...] += jnp.broadcast_to(c[Q - 1:Q], s_ref.shape)
    c2 = c * LOG2E
    cd = jnp.concatenate([c2, dt], 1)
    cd_ref[...] = cd
    cdt_ref[...] = cd.T
    f3 = _split3(dt * jnp.exp2(c2[Q - 1:Q] - c2))
    ea3 = _split3(jnp.exp2(c2[Q - 16:]))
    bt = xc_ref[:, E:E + N].astype(F32).T.astype(BF16)

    def body(j, _):
        L = _lanes(j, 256)
        ej = e_ref[:, L]
        xw = (xc_ref[:, L].astype(F32) * _dot(f3, ej)).astype(BF16)
        st = _dot(bt, xw)
        h = h_ref[:, L]
        hst_ref[:, L] = h
        h_ref[:, L] = h * _dot(ea3, ej)[15:16] + st
        return 0

    lax.fori_loop(0, E // 256, body, 0)


def _states(xc, dtr, bias, al, e64):
    t = xc.shape[0]
    nc = t // Q
    row = lambda w: pl.BlockSpec((Q, w), lambda i: (i, 0))
    return pl.pallas_call(
        _state_kernel,
        grid=(nc,),
        in_specs=[row(CD), row(H), _const((1, H)), _const((1, H)), _const((256, E))],
        out_specs=[row(2 * H), pl.BlockSpec((None, 2 * H, Q), lambda i: (i, 0, 0)),
                   pl.BlockSpec((None, N, E), lambda i: (i, 0, 0)), pl.BlockSpec((N, E), lambda i: (0, 0)),
                   pl.BlockSpec((8, H), lambda i: (0, 0))],
        out_shape=[jax.ShapeDtypeStruct((t, 2 * H), F32), jax.ShapeDtypeStruct((nc, 2 * H, Q), F32),
                   jax.ShapeDtypeStruct((nc, N, E), F32), jax.ShapeDtypeStruct((N, E), F32),
                   jax.ShapeDtypeStruct((8, H), F32)],
        compiler_params=_params(48),
        cost_estimate=_cost(25e9, 70e6),
        name='states',
    )(xc, dtr, bias, al, e64)


def _fwd_kernel(xc_ref, cd_ref, cdt_ref, hst_ref, hin_ref, z_ref, dyn_ref, d_ref, nw_ref, e_ref, e2_ref,
                yn_ref, dz_ref, dy_ref, hs_ref, dh_ref, gl_ref, row_ref, dnw_ref, dd_ref,
                y_s, sc_s, xm_s, cb_s, ece, acc1, acc2, p_hi, p_lo, q_s):
    i = pl.program_id(0)

    @pl.when(i == 0)
    def _():
        sc_s[...] = jnp.zeros_like(sc_s)
        ece[...] = jnp.ones_like(ece)
        gl_ref[...] = jnp.zeros_like(gl_ref)
        dnw_ref[...] = jnp.zeros_like(dnw_ref)
        dd_ref[...] = jnp.zeros_like(dd_ref)

    c2 = cd_ref[:, :H]
    c3 = _split3(c2)
    ec3 = _split3(jnp.exp2(c2))
    bm = xc_ref[:, E:E + N]
    cm = xc_ref[:, E + N:]
    ct = cm.astype(F32).T.astype(BF16)
    causal = _iota((Q, Q), 0) >= _iota((Q, Q), 1)
    cb_s[...] = jnp.where(causal, _nt(cm, bm), 0.0)
    acc1[...] = jnp.zeros_like(acc1)
    acc2[...] = jnp.zeros_like(acc2)
    head = _iota((1, 256), 1) // 64

    def quad(j, _):
        L = _lanes(j, 256)
        ej = e_ref[:, L]
        xq = xc_ref[:, L]
        ccol = _dot(c3, e2_ref[:, _lanes(j, 512)])
        h = hst_ref[:, L] + ece[0:1, L] * hin_ref[:, L]
        hs_ref[:, L] = h
        yi = _dot(cm, h.astype(BF16)) * _dot(ec3, ej)
        for k in range(4):
            crow = cdt_ref[pl.ds(4 * j + k, 1), :]
            drow = cdt_ref[pl.ds(H + 4 * j + k, 1), :]
            cc = ccol[:, k * 128:k * 128 + 128]
            for (a, b) in ((0, 0), (1, 0), (1, 1)):
                ra, rb = slice(a * HB, a * HB + HB), slice(b * HB, b * HB + HB)
                seg = jnp.minimum(cc[ra] - crow[:, rb], 0.0)
                w = jnp.exp2(seg) * drow[:, rb]
                sc_s[ra, k * Q + b * HB:k * Q + b * HB + HB] = (cb_s[ra, rb] * w).astype(BF16)
            xm_s[k * Q:k * Q + Q, :] = jnp.where(head == k, xq, jnp.zeros_like(xq))
        y = yi + _dot(sc_s[...], xm_s[...])
        y_s[:, L] = y
        z = z_ref[:, L].astype(F32)
        g = (y + d_ref[:, L] * xq.astype(F32)) * (z * jax.nn.sigmoid(z))
        gg = g * g
        gd = g * (dyn_ref[:, L].astype(F32) * nw_ref[:, L])
        acc1[...] += gg[:, :128] + gg[:, 128:]
        acc2[...] += gd[:, :128] + gd[:, 128:]
        return 0

    lax.fori_loop(0, E // 256, quad, 0)
    r = lax.rsqrt(jnp.sum(acc1[...], 1, keepdims=True) / E + EPS)
    m = jnp.sum(acc2[...], 1, keepdims=True) / E * (r * r * r)
    acc1[...] = jnp.broadcast_to(r, acc1.shape)
    acc2[...] = jnp.broadcast_to(m, acc2.shape)
    row_ref[...] = jnp.zeros_like(row_ref)
    RB = 64

    def gate(j, _):
        L = _lanes(j, 256)
        ej = e_ref[:, L]
        ecq = _dot(ec3, ej)
        q_s[...] = ecq

        def rows(k, _):
            R = pl.ds(pl.multiple_of(k * RB, RB), RB)
            x = xc_ref[R, L].astype(F32)
            ys = y_s[R, L]
            y = ys + d_ref[:, L] * x
            z = z_ref[R, L].astype(F32)
            sg = jax.nn.sigmoid(z)
            sz = z * sg
            g = y * sz
            rb = jnp.concatenate([acc1[R, :], acc1[R, :]], 1)
            mb = jnp.concatenate([acc2[R, :], acc2[R, :]], 1)
            gr = g * rb
            dn = dyn_ref[R, L].astype(F32)
            nw = nw_ref[:, L]
            yn_ref[R, L] = (gr * nw).astype(BF16)
            dnw_ref[:, L] += jnp.sum((dn * gr).reshape(RB // 8, 8, 256), 0)
            dg = rb * (dn * nw) - g * mb
            dy = dg * sz
            dz_ref[R, L] = (dg * y * (sg + sz * (1.0 - sg))).astype(BF16)
            dy_ref[R, L] = dy
            dd_ref[:, L] += jnp.sum((dy * x).reshape(RB // 8, 8, 256), 0)
            hi, lo = _split2(dy.astype(BF16).astype(F32) * ys)
            p_hi[R, :] = hi
            p_lo[R, :] = lo
            q_s[R, :] = q_s[R, :] * dy
            return 0

        lax.fori_loop(0, Q // RB, rows, 0)
        er = e_ref[0:2 * H, L]
        row_ref[...] += _nt(p_hi[...], er) + _nt(p_lo[...], er)
        dh = _dot(ct, q_s[...].astype(BF16)).astype(BF16)
        dh_ref[:, L] = dh
        gl_ref[:, L] += ece[0:1, L] * dh.astype(F32)
        ece[:, L] = ece[:, L] * ecq[Q - 1:Q]
        return 0

    lax.fori_loop(0, E // 256, gate, 0)


def _fwd(xc, cd, cdt, hst, hin, z, dyn, dx, nw, e64, e128):
    t = xc.shape[0]
    nc = t // Q
    row = lambda w: pl.BlockSpec((Q, w), lambda i: (i, 0))
    blk = lambda a, b: pl.BlockSpec((None, a, b), lambda i: (i, 0, 0))
    fix = lambda a, b: pl.BlockSpec((a, b), lambda i: (0, 0))
    return pl.pallas_call(
        _fwd_kernel,
        grid=(nc,),
        in_specs=[row(CD), row(2 * H), blk(2 * H, Q), blk(N, E), _const((N, E)), row(E), row(E), _const((1, E)),
                  _const((1, E)), _const((256, E)), _const((256, 2 * E))],
        out_specs=[row(E), row(E), row(E), blk(N, E), blk(N, E), fix(N, E), row(2 * H), fix(8, E), fix(8, E)],
        out_shape=[jax.ShapeDtypeStruct((t, E), BF16), jax.ShapeDtypeStruct((t, E), BF16),
                   jax.ShapeDtypeStruct((t, E), F32), jax.ShapeDtypeStruct((nc, N, E), F32),
                   jax.ShapeDtypeStruct((nc, N, E), BF16), jax.ShapeDtypeStruct((N, E), F32),
                   jax.ShapeDtypeStruct((t, 2 * H), F32), jax.ShapeDtypeStruct((8, E), F32),
                   jax.ShapeDtypeStruct((8, E), F32)],
        scratch_shapes=[pltpu.VMEM((Q, E), F32), pltpu.VMEM((Q, 4 * Q), BF16), pltpu.VMEM((4 * Q, 256), BF16),
                        pltpu.VMEM((Q, Q), F32), pltpu.VMEM((8, E), F32), pltpu.VMEM((Q, 128), F32),
                        pltpu.VMEM((Q, 128), F32), pltpu.VMEM((Q, 256), BF16), pltpu.VMEM((Q, 256), BF16),
                        pltpu.VMEM((Q, 256), F32)],
        compiler_params=_params(60),
        cost_estimate=_cost(150e9, 270e6),
        name='ssd_fwd_gate',
    )(xc, cd, cdt, hst, hin, z, dyn, dx, nw, e64, e128)


def _bwd_kernel(xc_ref, cd_ref, cdt_ref, hs_ref, dh_ref, gin_ref, dae_ref, dy_ref, row_ref, d_ref, dtr_ref, bias_ref,
                al_ref, e_ref, e2_ref,
                dxc_ref, ddtr_ref, red_ref,
                g_s, sc_s, xm_s, dm_s, cb_s, w_s, dcb_s, dae_s, col_s, db_s, dc_s):
    i = pl.program_id(0)

    @pl.when(i == 0)
    def _():
        sc_s[...] = jnp.zeros_like(sc_s)
        g_s[...] = gin_ref[...]
        dae_s[...] = dae_ref[...]
        red_ref[...] = jnp.zeros_like(red_ref)

    c2 = cd_ref[:, :H]
    dt = cd_ref[:, H:]
    c3 = _split3(c2)
    d3 = _split3(dt)
    ec3 = _split3(jnp.exp2(c2))
    f3 = _split3(dt * jnp.exp2(c2[Q - 1:Q] - c2))
    bm = xc_ref[:, E:E + N]
    cm = xc_ref[:, E + N:]
    causal = _iota((Q, Q), 0) <= _iota((Q, Q), 1)
    cb_s[...] = jnp.where(causal, _nt(bm, cm), 0.0)
    dcb_s[...] = jnp.zeros_like(dcb_s)
    col_s[...] = jnp.zeros_like(col_s)
    db_s[...] = jnp.zeros_like(db_s)
    dc_s[...] = jnp.zeros_like(dc_s)
    head = _iota((1, 256), 1) // 64
    er0 = e_ref[0:2 * H, :]
    dae = dae_s[...]
    dhi = dae.astype(BF16)
    dmid = (dae - dhi.astype(F32)).astype(BF16)
    dlo = (dae - dhi.astype(F32) - dmid.astype(F32)).astype(BF16)
    dae_h = (_nt(dhi, er0) + _nt(dmid, er0) + _nt(dlo, er0))[0:1, :H]

    def quad(j, _):
        L = _lanes(j, 256)
        ej = e_ref[:, L]
        xq = xc_ref[:, L]
        dy = dy_ref[:, L]
        dyb = dy.astype(BF16)
        for k in range(4):
            sel = head == k
            xm_s[k * Q:k * Q + Q, :] = jnp.where(sel, xq, jnp.zeros_like(xq))
            dm_s[k * Q:k * Q + Q, :] = jnp.where(sel, dyb, jnp.zeros_like(dyb))
        e2j = e2_ref[:, _lanes(j, 512)]
        ccol = _dot(c3, e2j)
        dcol = _dot(d3, e2j)
        w_s[...] = _nt(xm_s[...], dyb)
        for k in range(4):
            crow = cdt_ref[pl.ds(4 * j + k, 1), :]
            cc = ccol[:, k * 128:k * 128 + 128]
            dc = dcol[:, k * 128:k * 128 + 128]
            for (a, b) in ((0, 0), (0, 1), (1, 1)):
                ra, rb = slice(a * HB, a * HB + HB), slice(b * HB, b * HB + HB)
                seg = jnp.minimum(crow[:, rb] - cc[ra], 0.0)
                w = jnp.exp2(seg) * dc[ra]
                sc_s[ra, k * Q + b * HB:k * Q + b * HB + HB] = (cb_s[ra, rb] * w).astype(BF16)
                ds = w_s[k * Q + a * HB:k * Q + a * HB + HB, rb].astype(BF16).astype(F32)
                dcb_s[ra, rb] += ds * w
        dxs = _dot(sc_s[...], dm_s[...])
        fq = _dot(f3, ej)
        g = g_s[:, L]
        gb = g.astype(BF16)
        x = xq.astype(F32)
        dxw = _dot(bm, gb).astype(BF16).astype(F32)
        dxs = dxs + fq * dxw
        db_s[...] += _nt((x * fq).astype(BF16), gb)
        ecq = _dot(ec3, ej)
        hs = hs_ref[:, L]
        dc_s[...] += _nt((ecq * dy).astype(BF16), hs.astype(BF16))
        hi, lo = _split2(x * dxs)
        er = e_ref[0:2 * H, L]
        col_s[...] += _nt(hi, er) + _nt(lo, er)
        dxc_ref[:, L] = (dxs + d_ref[:, L] * dy).astype(BF16)
        gn = g * ecq[Q - 1:Q] + dh_ref[:, L].astype(F32)
        g_s[:, L] = gn
        dae_s[:, L] = jnp.broadcast_to(jnp.sum(gn * hs, 0, keepdims=True), (8, 256))
        return 0

    lax.fori_loop(0, E // 256, quad, 0)
    dcb = jnp.where(causal, dcb_s[...], 0.0)
    dxc_ref[:, E:E + N] = (db_s[...] + _dot(dcb.astype(BF16), cm)).astype(BF16)
    dxc_ref[:, E + N:] = (dc_s[...] + _dot(dcb.T.astype(BF16), bm)).astype(BF16)

    col = col_s[:, :H]
    dcs = row_ref[:, :H] - col
    dcs = dcs + jnp.where(_iota((Q, H), 0) == Q - 1, dae_h, 0.0)
    triu = (_iota((Q, Q), 0) <= _iota((Q, Q), 1)).astype(F32)
    da = lax.dot_general(triu, dcs, (((1,), (0,)), ((), ())), precision=HI, preferred_element_type=F32)
    na = -jnp.exp(al_ref[...])
    ddt = jnp.where(dt > 0.0, col / jnp.where(dt > 0.0, dt, 1.0), 0.0) + da * na
    ddtr = ddt * jax.nn.sigmoid(dtr_ref[...].astype(F32) + bias_ref[...])
    ddtr_ref[...] = ddtr.astype(BF16)
    both = jnp.concatenate([ddtr, da * (na * dt)], 1)
    red_ref[...] += jnp.sum(both.reshape(Q // 8, 8, 2 * H), 0)


def _bwd(xc, cd, cdt, hs, dh, gin, dae, dy, row, dx, dtr, bias, al, e64, e128):
    t = xc.shape[0]
    nc = t // Q
    rows = lambda w: pl.BlockSpec((Q, w), lambda i: (nc - 1 - i, 0))
    blk = lambda a, b: pl.BlockSpec((None, a, b), lambda i: (nc - 1 - i, 0, 0))
    fix = lambda a, b: pl.BlockSpec((a, b), lambda i: (0, 0))
    return pl.pallas_call(
        _bwd_kernel,
        grid=(nc,),
        in_specs=[rows(CD), rows(2 * H), blk(2 * H, Q), blk(N, E), blk(N, E), _const((N, E)), _const((8, E)), rows(E),
                  rows(2 * H), _const((1, E)), rows(H), _const((1, H)), _const((1, H)), _const((256, E)),
                  _const((256, 2 * E))],
        out_specs=[rows(CD), rows(H), fix(8, 2 * H)],
        out_shape=[jax.ShapeDtypeStruct((t, CD), BF16), jax.ShapeDtypeStruct((t, H), BF16),
                   jax.ShapeDtypeStruct((8, 2 * H), F32)],
        scratch_shapes=[pltpu.VMEM((N, E), F32), pltpu.VMEM((Q, 4 * Q), BF16), pltpu.VMEM((4 * Q, 256), BF16),
                        pltpu.VMEM((4 * Q, 256), BF16), pltpu.VMEM((Q, Q), F32), pltpu.VMEM((4 * Q, Q), F32),
                        pltpu.VMEM((Q, Q), F32), pltpu.VMEM((8, E), F32), pltpu.VMEM((Q, 2 * H), F32),
                        pltpu.VMEM((Q, N), F32), pltpu.VMEM((Q, N), F32)],
        compiler_params=_params(60),
        cost_estimate=_cost(150e9, 220e6),
        name='ssd_bwd',
    )(xc, cd, cdt, hs, dh, gin, dae, dy, row, dx, dtr, bias, al, e64, e128)


def _prefix(s):
    k = s.shape[0]
    cs = jnp.cumsum(s, 0)
    diff = (cs - s)[:, None] - cs[None, :]
    m = (jnp.arange(k)[:, None] > jnp.arange(k)[None, :]).reshape((k, k) + (1,) * (s.ndim - 1))
    return jnp.where(m, jnp.exp(jnp.where(m, diff, 0.0)), 0.0)


def _wide(v):
    return jnp.repeat(v, E // H, axis=-1)


def solution(mesh):
    nseq = mesh.shape['seq']
    fwd = [(i, i + 1) for i in range(nseq - 1)]
    bwd = [(i + 1, i) for i in range(nseq - 1)]
    core = [(i, i ^ 1) for i in range(nseq)]
    chip = [(i, i ^ 2) for i in range(nseq)]

    def local(x, dout, W_in, conv_w, conv_b, dt_bias, A_log, D_skip, norm_w, W_out):
        t, dm = x.shape
        idx = lax.axis_index('seq')
        c, k = idx % 2, idx // 2
        rows = jnp.arange(256)
        lane = jnp.arange(2 * E)
        e128 = ((rows[:, None] % H == lane[None, :] // 128) & (rows[:, None] < 3 * H)).astype(BF16)
        e64 = ((rows[:, None] % H == lane[None, :E] // 64) & (rows[:, None] < 3 * H)).astype(BF16)
        bias, al = dt_bias[None], A_log[None]
        dwide = _wide(D_skip)[None]
        Wz, Wx = W_in[:, :E], W_in[:, E:]

        xb = jnp.dot(x, Wx, preferred_element_type=F32).astype(BF16)
        halo = lax.ppermute(xb[t - 16:], 'seq', fwd)
        dtr = xb[:, CD:]
        xc = _conv_fwd(xb, halo, conv_w, conv_b[None])
        cd, cdt, hst, h_loc, s8 = _states(xc, dtr, bias, al, e64)
        s = s8[0]
        s_all = lax.all_gather(s, 'seq')
        h_all = lax.all_gather(h_loc, 'seq')
        wd = _wide(_prefix(s_all))
        h_in = jnp.sum(wd[idx][:, None, :] * h_all, 0)
        h_fin = h_loc + _wide(jnp.exp(s))[None] * h_in
        z = jnp.dot(x, Wz, preferred_element_type=F32).astype(BF16)
        dyn = _nt(dout, W_out).astype(BF16)
        yn, dz, dy, hs, dh, g_loc, row, dnw8, dd8 = _fwd(xc, cd, cdt, hst, h_in, z, dyn, dwide, norm_w[None], e64, e128)
        g_all = lax.all_gather(g_loc, 'seq')

        def quarters(a):
            w = a.shape[1] // 4
            cut = lambda cc, kk: lax.dynamic_slice_in_dim(a, (2 * cc + kk) * w, w, 1)
            return (jnp.concatenate([cut(1 - c, 1 - k), cut(1 - c, k)], 1), cut(c, 1 - k), cut(c, k))

        xs, ds = quarters(x), quarters(dout)

        def spread(mine):
            other = lax.ppermute(mine, 'seq', chip)
            mine_p = lax.ppermute(mine, 'seq', core)
            other_p = lax.ppermute(other, 'seq', core)
            return [(2 * c + k, mine), (2 * c + 1 - k, other), (2 - 2 * c + k, mine_p), (3 - 2 * c - k, other_p)]

        sO = _tn(yn, ds[0])
        rO = lax.ppermute(sO, 'seq', core)
        sZ = _tn(xs[0], dz)
        rZ = lax.ppermute(sZ, 'seq', core)
        dh_fin = jnp.sum(wd[:, idx][:, None, :] * g_all, 0)
        dae = jnp.broadcast_to(jnp.sum(dh_fin * h_fin, 0)[None], (8, E))
        w4 = dm // 4
        fO = _tn(yn, ds[1]) + rO[:, :w4]
        fZ = _tn(xs[1], dz) + rZ[:w4]
        fO, fZ, dy, dae = lax.optimization_barrier((fO, fZ, dy, dae))
        gO = lax.ppermute(fO, 'seq', chip)
        gZ = lax.ppermute(fZ, 'seq', chip)
        oO = _tn(yn, ds[2]) + rO[:, w4:]
        oZ = _tn(xs[2], dz) + rZ[w4:]
        dxc, ddtr, red = _bwd(xc, cd, cdt, hs, dh, dh_fin, dae, dy, row, dwide, dtr, bias, al, e64, e128)
        dxc, gO, gZ, oO, oZ = lax.optimization_barrier((dxc, gO, gZ, oO, oZ))
        pO = spread((oO + gO).astype(BF16))
        pZ = spread((oZ + gZ).astype(BF16))
        dxb, gw8, gb8, head, tail = _conv_bwd(xb, halo, dxc, conv_w, conv_b[None])
        nxt = lax.ppermute(head, 'seq', bwd)
        fix = sum(conv_w[j] * jnp.pad(nxt[:j], ((16 - j, 0), (0, 0))) for j in range(1, KCONV))
        dxb = lax.dynamic_update_slice(dxb, (tail + fix).astype(BF16), (t - 16, 0))
        dxb = lax.dynamic_update_slice(dxb, ddtr, (0, CD))

        dcw = jnp.sum(gw8.reshape(KCONV, 8, CD), 1)
        small = jnp.concatenate([dcw.reshape(-1), jnp.sum(gb8, 0), jnp.sum(red, 0), jnp.sum(dd8, 0).reshape(H, E // H).sum(1),
                                 jnp.sum(dnw8, 0)])
        small = small + lax.ppermute(small, 'seq', core)
        small = small + lax.ppermute(small, 'seq', chip)

        sX = _tn(xs[0], dxb)
        rX = lax.ppermute(sX, 'seq', core)
        fX = _tn(xs[1], dxb) + rX[:w4]
        fX, small = lax.optimization_barrier((fX, small))
        gX = lax.ppermute(fX, 'seq', chip)
        oX = _tn(xs[2], dxb) + rX[w4:]
        dx0 = _nt(dz, Wz)
        pX = spread((oX + gX).astype(BF16))
        dx = (dx0 + _nt(dxb, Wx)).astype(BF16)

        def place(out, pieces, axis, col=0):
            for pos, p in pieces:
                w = p.shape[axis]
                at = (pos * w, jnp.int32(col)) if axis == 0 else (jnp.int32(0), pos * w)
                out = lax.dynamic_update_slice(out, p, at)
            return out

        dW_in = place(place(jnp.zeros((dm, E + PX), BF16), pZ, 0), pX, 0, E)
        dW_out = place(jnp.zeros((E, dm), BF16), pO, 1)
        cuts = []
        for n in (KCONV * CD, CD, H, H, H, E):
            cuts.append(small[:n])
            small = small[n:]
        dcw, dcb, ddtb, dal, dD, dnw = cuts
        dcw = dcw.reshape(KCONV, CD)
        return dx, dW_in, dcw, dcb, ddtb, dal, dD, dnw, dW_out

    xs = P(('data', 'seq'), None)
    return jax.shard_map(local, mesh=mesh, in_specs=(xs, xs) + (P(),) * 8,
                         out_specs=(xs, P('data', None), P('data', None), P('data'), P('data'), P('data'),
                                    P('data'), P('data'), P('data', None)),
                         check_vma=False)
```

time: 5560 us -> 2200 us (0.40)
  blocking collectives: 1740 us -> 8.64 us
  other arithmetic: 1210 us -> 57.2 us
  Pallas kernels: 0 us -> 1000 us
  local copies, waits for them, and re-layouts: 1050 us -> 113 us
  matrix products: 1500 us -> 714 us
  waiting for transfers between devices: 0.08 us -> 268 us
    psum x1 -> x0, blocking collectives: 1730 us -> none  [local(): lax.psum((dW_in, dcw, dcb, ddtb, dal, dD, dnw, dW_out), 'seq')]
    pallas_call x0 -> x5, Pallas kernels: none -> 1000 us  [the longest x1 396 us: _fwd(): pl.pallas_call(_fwd_kernel, grid=(nc,), in_specs=[row(CD), row(2 * H), bl...]
    dot_general x16 -> x2, matrix products: 961 us -> 166 us  [the longest x1 88.9 us: local(): xb = jnp.dot(x, Wx, preferred_element_type=F32).astype(BF16)]
    reduce_sum x17 -> x9, other arithmetic: 724 us -> 13.9 us  [the longest x1 6.04 us: local(): h_in = jnp.sum(wd[idx][:, None, :] * h_all, 0)]
    reshape x11 -> x4, local copies, waits for them, and re-layouts: 579 us -> 0.99 us  [the longest x1 0.66 us: local(): dcw = dcw.reshape(KCONV, CD)]
    ppermute x2 -> x19, waiting for transfers between devices: 0.01 us -> 268 us  [the longest x1 134 us: local(): gX = lax.ppermute(fX, 'seq', chip)]
    convert_element_type x5 -> x3, other arithmetic: 257 us -> 14.9 us  [the longest x1 9 us: local(): pZ = spread((oZ + gZ).astype(BF16))]
    convert_element_type x3 -> x1, local copies, waits for them, and re-layouts: 209 us -> 6.45 us  [local(): pZ = spread((oZ + gZ).astype(BF16))]
  transfers between devices with their start and end apart: 5 -> 21, of which waited for: 0 -> 5; matrix products, arithmetic and copies ran while one was open for 16% -> 32% of each run, Pallas kernels for 0% -> 14%
where the time goes in v1:
time: 2200 us; the launch traced here: 2190 us
  Pallas kernels  1000 us (45%)
  matrix products  714 us (32%)
  waiting for transfers between devices  268 us (12%)
  local copies, waits for them, and re-layouts  113 us (5%)
  other arithmetic  57.2 us (3%)
    pallas_call x1, Pallas kernels, _fwd(): pl.pallas_call(_fwd_kernel, grid=(nc,), in_specs=[row(CD), row(2 * H), bl...  396 us
    pallas_call x1, Pallas kernels, _bwd(): pl.pallas_call(_bwd_kernel, grid=(nc,), in_specs=[rows(CD), rows(2 * H),...  308 us
    dot_general x9, matrix products, _tn(): lax.dot_general(a, b, (((0,), (0,)), ((), ())), preferred_element_type=F32)  302 us
    dot_general x3, matrix products, _nt(): lax.dot_general(a, b, (((1,), (1,)), ((), ())), preferred_element_type=F32)  245 us
    ppermute x1, waiting for transfers between devices, local(): gX = lax.ppermute(fX, 'seq', chip)  134 us
    pallas_call x1, Pallas kernels, _conv_bwd(): pl.pallas_call(_conv_bwd_kernel, grid=(CD // cw,), in_specs=[col(t), col(...  131 us
    pallas_call x1, Pallas kernels, _states(): pl.pallas_call(_state_kernel, grid=(nc,), in_specs=[row(CD), row(H), _con...  116 us
    ppermute x3, waiting for transfers between devices, spread(): other = lax.ppermute(mine, 'seq', chip)  106 us
  transfers between devices with their start and end apart: 21, of which 5 were waited for; matrix products, arithmetic and copies ran while one was open for 32% of the time, Pallas kernels for 14%

profile of v1, /device:TPU:0, one launch (start us, length us, event | category | flops | bytes accessed | tf_op | source)
XLA Modules:
  0.0 2192.1 jit_solution(14357458109836066955)
XLA Ops:
  7.2 88.9 %convolution_convert_fusion.x_ref = bf16[4096,4416]{1,0:T(8,128)(2,1)} fusion(bf16[4096,2048]{1,0:T(8,128)(2,1)} %param.10, bf16[2048,8512]{0,1:T(8,128)(2,1)} %param.12), kind=kOutput, calls=%fused_computation | convolution fusion | flops 74106273792 | bytes 71041024 | tf_op jit(solution)/shard_map/dot_general | solution.py:501
  96.1 1.6 slice.112
  97.7 3.8 collective-permute-start
  103.2 77.5 %convolution_convert_fusion.2.z_ref = bf16[4096,4096]{1,0:T(8,128)(2,1)} fusion(bf16[4096,2048]{1,0:T(8,128)(2,1)} %param.10, bf16[2048,8512]{0,1:T(8,128)(2,1)} %param.12), kind=kOutput, calls=%fused_computation.3 | convolution fusion | flops 68736253952 | bytes 67108864 | tf_op jit(solution)/shard_map/dot_general | solution.py:512
  180.9 2.2 and_convert_fusion.1.e_ref
  183.1 3.7 and_convert_fusion.e2_ref
  186.8 12.4 constant_dynamic-slice_fusion.1
  199.2 1.3 slice.113.dtr_ref
  200.6 0.8 broadcast_in_dim_reshape.4.d_ref
  202.0 50.1 %conv_fwd.1.xc_ref = bf16[4096,4352]{1,0:T(8,128)(2,1)} custom-call(bf16[4096,4416]{1,0:T(8,128)(2,1)} %convolution_convert_fusion.x_ref, bf16[16,4416]{1,0:T(8,128)(2,1)} %collective-permute-done.halo_ref, f32[4,4352]{1,0:T(4,128)S(1)} %copy-done.1, f32[1,4352]{1,0:T(1,128)S(1)} %broadcast_in_dim.62.b_ref), custom_call_target="tpu_custom_call" | custom-call | flops 24999999488 | bytes 71303168 | tf_op jit(solution)/shard_map/conv_fwd/pallas_call | solution.py:93
  252.0 115.8 %states.1 = (f32[4096,128]{1,0:T(8,128)S(1)}, f32[16,128,256]{2,1,0:T(8,128)S(1)}, f32[16,128,4096]{2,1,0:T(8,128)}, f32[128,4096]{1,0:T(8,128)}, f32[8,64]{1,0:T(8,128)S(1)}) custom-call(bf16[4096,4352]{1,0:T(8,128)(2,1)} %conv_fwd.1.xc_ref, bf16[4096,64]{1,0:T(8,128)(2,1)S(1)} %slice.113.dtr_ref, f32[1,64]{1,0:T(1,128)S(1)} %bitcast.41, ...), custom_call_target="tpu_custom_call" | custom-call | flops 24999999488 | bytes 70000000 | tf_op jit(solution)/shard_map/states/pallas_call | solution.py:198
  367.8 1.3 copy-done.4
  369.1 1.4 copy-done.5
  370.8 77.7 %convolution_convert_fusion.1.dyn_ref = bf16[4096,4096]{1,0:T(8,128)(2,1)} fusion(bf16[4096,2048]{1,0:T(8,128)(2,1)} %param.11, bf16[4096,2048]{1,0:T(8,128)(2,1)} %param.19), kind=kOutput, calls=%fused_computation.2 | convolution fusion | flops 68736253952 | bytes 67108864 | tf_op jit(solution)/shard_map/dot_general | solution.py:32
  449.0 8.6 all-gather.2
  458.4 6.0 multiply_reduce_fusion.1.hin_ref
  464.4 395.8 %ssd_fwd_gate.1 = (bf16[4096,4096]{1,0:T(8,128)(2,1)}, bf16[4096,4096]{1,0:T(8,128)(2,1)}, f32[4096,4096]{1,0:T(8,128)}, f32[16,128,4096]{2,1,0:T(8,128)}, bf16[...) custom-call(bf16[4096,4352]{1,0:T(8,128)(2,1)} %conv_fwd.1.xc_ref, ...), custom_call_target="tpu_custom_call" | custom-call | flops 149999992832 | bytes 270000000 | tf_op jit(solution)/shard_map/ssd_fwd_gate/pallas_call | solution.py:326
  860.2 43.8 %fusion.7 = f32[4096,1024]{1,0:T(8,128)} fusion(bf16[4096,4096]{1,0:T(8,128)(2,1)} %get-tuple-element.51, bf16[4096,512]{1,0:T(8,128)(2,1)} %get-tuple-element.91, bf16[4096,512]{1,0:T(8,128)(2,1)} %get-tuple-element.92), kind=kOutput, calls=%fused_computation.17 | convolution fusion | flops 34376515584 | bytes 58720256 | tf_op jit(solution)/shard_map/dot_general | solution.py:28
  904.0 43.0 %fusion.12 = f32[1024,4096]{1,0:T(8,128)} fusion(bf16[4096,4096]{1,0:T(8,128)(2,1)} %get-tuple-element.47, bf16[4096,512]{1,0:T(8,128)(2,1)} %get-tuple-element.83, bf16[4096,512]{1,0:T(8,128)(2,1)S(1)} %copy-done.9), kind=kOutput, calls=%fused_computation.28 | convolution fusion | flops 34376515584 | bytes 58720256 | tf_op jit(solution)/shard_map/dot_general | solution.py:28
  947.7 0.8 dynamic-slice_bitcast_fusion
  948.5 4.6 multiply_reduce_fusion.gin_ref
  953.2 2.8 multiply_reduce_fusion.2
  956.0 28.3 %slice_add_fusion.5 = f32[4096,512]{1,0:T(8,128)} fusion(f32[4096,1024]{1,0:T(8,128)} %collective-permute-done.1, bf16[4096,4096]{1,0:T(8,128)(2,1)} %get-tuple-element.51, bf16[4096,2048]{1,0:T(8,128)(2,1)} %param.11, s32[]{:T(128)S(6)} %select_n.107), kind=kOutput, calls=%fused_computation.16 | convolution fusion | flops 17181966336 | bytes 54525956 | tf_op jit(solution)/shard_map/dot_general | solution.py:28
  984.4 28.3 %slice_add_fusion.4 = f32[512,4096]{1,0:T(8,128)} fusion(f32[1024,4096]{1,0:T(8,128)} %collective-permute-done.2, bf16[4096,4096]{1,0:T(8,128)(2,1)} %get-tuple-element.47, bf16[4096,2048]{1,0:T(8,128)(2,1)} %param.10, s32[]{:T(128)S(6)} %select_n.107), kind=kOutput, calls=%fused_computation.15 | convolution fusion | flops 17181966336 | bytes 54525956 | tf_op jit(solution)/shard_map/dot_general | solution.py:28
  1013.4 2.0 collective-permute-start.4
  1015.4 307.8 %ssd_bwd.1 = (bf16[4096,4352]{1,0:T(8,128)(2,1)}, bf16[4096,64]{1,0:T(8,128)(2,1)}, f32[8,128]{1,0:T(8,128)}) custom-call(bf16[4096,4352]{1,0:T(8,128)(2,1)} %conv_fwd.1.xc_ref, f32[4096,128]{1,0:T(8,128)} %copy-done.4, f32[16,128,256]{2,1,0:T(8,128)} %copy-done.5, f32[16,128,4096]{2,1,0:T(8,128)} %get-tuple-element.48.hs_ref, ...), custom_call_target="tpu_custom_call" | custom-call | flops 149999992832 | bytes 220000000 | tf_op jit(solution)/shard_map/ssd_bwd/pallas_call | solution.py:451
  1323.2 28.4 %slice_add_fusion.2 = f32[512,4096]{1,0:T(8,128)} fusion(f32[1024,4096]{1,0:T(8,128)} %collective-permute-done.2, bf16[4096,4096]{1,0:T(8,128)(2,1)} %get-tuple-element.47, bf16[4096,2048]{1,0:T(8,128)(2,1)} %param.10, s32[]{:T(128)S(6)} %select_n.110), kind=kOutput, calls=%fused_computation.13 | convolution fusion | flops 17181966336 | bytes 54525956 | tf_op jit(solution)/shard_map/dot_general | solution.py:28
  1351.6 28.5 %slice_add_fusion.3 = f32[4096,512]{1,0:T(8,128)} fusion(f32[4096,1024]{1,0:T(8,128)} %collective-permute-done.1, bf16[4096,4096]{1,0:T(8,128)(2,1)} %get-tuple-element.51, bf16[4096,2048]{1,0:T(8,128)(2,1)} %param.11, s32[]{:T(128)S(6)} %select_n.110), kind=kOutput, calls=%fused_computation.14 | convolution fusion | flops 17181966336 | bytes 54525956 | tf_op jit(solution)/shard_map/dot_general | solution.py:28
  1380.2 130.9 %conv_bwd.1 = (bf16[4096,4416]{1,0:T(8,128)(2,1)}, f32[32,4352]{1,0:T(8,128)S(1)}, f32[8,4352]{1,0:T(8,128)S(1)}, f32[8,4352]{1,0:T(8,128)S(1)}, f32[16,4352]{1,0:T(8,128)S(1)}) custom-call(bf16[4096,4416]{1,0:T(8,128)(2,1)} %convolution_convert_fusion.x_ref, bf16[16,4416]{1,0:T(8,128)(2,1)} %collective-permute-done.halo_ref, ...), custom_call_target="tpu_custom_call" | custom-call | flops 49999998976 | bytes 106954752 | tf_op jit(solution)/shard_map/conv_bwd/pallas_call | solution.py:145
  1511.1 1.3 collective-permute-start.5
  1512.5 1.8 collective-permute-done.5
  1515.1 1.1 constant_dynamic-update-slice_fusion.8
  1516.3 46.6 %fusion.11 = f32[1024,4416]{0,1:T(8,128)} fusion(bf16[4096,4416]{1,0:T(8,128)(2,1)} %constant_dynamic-update-slice_fusion.8, bf16[4096,512]{1,0:T(8,128)(2,1)} %get-tuple-element.83, bf16[4096,512]{1,0:T(8,128)(2,1)} %get-tuple-element.82), kind=kOutput, calls=%fused_computation.27 | convolution fusion | flops 37060870144 | bytes 62652416 | tf_op jit(solution)/shard_map/dot_general | solution.py:28
  1562.9 2.7 collective-permute-start.9
  1566.2 26.2 %collective-permute-done.10 = f32[26048]{0:T(1024)S(1)} collective-permute-done((f32[26048]{0:T(1024)S(1)}, f32[26048]{0:T(1024)S(1)}, u32[]{:S(2)}, u32[]{:S(2)}) %collective-permute-start.10) | collective-permute-done | bytes 104224 | tf_op jit(solution)/shard_map/ppermute | solution.py:557
  1592.5 9.0 add_convert_fusion.2
  1601.5 1.9 collective-permute-start.6
  1604.1 27.9 %slice_add_fusion = f32[512,4416]{0,1:T(8,128)} fusion(f32[1024,4416]{0,1:T(8,128)} %collective-permute-done.9, bf16[4096,4416]{1,0:T(8,128)(2,1)} %constant_dynamic-update-slice_fusion.8, bf16[4096,2048]{1,0:T(8,128)(2,1)} %param.10, s32[]{:T(128)S(6)} %select_n.107), kind=kOutput, calls=%fused_computation.9 | convolution fusion | flops 18524307456 | bytes 58982404 | tf_op jit(solution)/shard_map/dot_general | solution.py:28
  1632.0 6.5 copy.30
  1638.5 6.1 broadcast_in_dim.73
  1644.6 10.7 constant_dynamic-update-slice_fusion.3
  1655.2 2.0 collective-permute-start.16
  1657.4 11.6 broadcast_in_dim.72
  1669.0 2.3 constant_dynamic-update-slice_fusion.7
  1671.3 23.7 %collective-permute-done.6 = bf16[512,4096]{1,0:T(8,128)(2,1)} collective-permute-done((bf16[512,4096]{1,0:T(8,128)(2,1)}, bf16[512,4096]{1,0:T(8,128)(2,1)}, u32[]{:S(2)}, u32[]{:S(2)}) %collective-permute-start.6) | collective-permute-done | bytes 4194336 | tf_op jit(solution)/shard_map/ppermute | solution.py:525
  1695.0 27.1 %fusion.15 = f32[512,4416]{0,1:T(8,128)} fusion(bf16[4096,4416]{1,0:T(8,128)(2,1)} %constant_dynamic-update-slice_fusion.8, bf16[4096,2048]{1,0:T(8,128)(2,1)} %param.10, s32[]{:T(128)S(6)} %select_n.110), kind=kOutput, calls=%fused_computation.32 | convolution fusion | flops 18522046464 | bytes 49938436 | tf_op jit(solution)/shard_map/dot_general | solution.py:28
  1722.1 6.5 copy.31
  1728.6 6.5 copy.32
  1735.1 4.5 constant_dynamic-update-slice_fusion.6
  1739.6 4.5 constant_dynamic-update-slice_fusion.5
  1744.1 6.5 copy.33
  1750.6 4.5 constant_dynamic-update-slice_fusion.4
  1755.0 133.7 %collective-permute-done.12 = f32[512,4416]{0,1:T(8,128)} collective-permute-done((f32[512,4416]{0,1:T(8,128)}, f32[512,4416]{0,1:T(8,128)}, u32[]{:S(2)}, u32[]{:S(2)}) %collective-permute-start.12) | collective-permute-done | bytes 9044000 | tf_op jit(solution)/shard_map/ppermute | solution.py:564
  1888.8 13.9 constant_dynamic-update-slice_fusion.12
  1902.7 1.9 collective-permute-start.13
  1904.6 87.5 %fusion = f32[4096,2048]{1,0:T(8,128)} fusion(bf16[4096,4416]{1,0:T(8,128)(2,1)} %constant_dynamic-update-slice_fusion.8, bf16[2048,8512]{0,1:T(8,128)(2,1)} %param.12), kind=kOutput, calls=%fused_computation.4 | convolution fusion | flops 74088185856 | bytes 88342528 | tf_op jit(solution)/shard_map/dot_general | solution.py:32
  1992.6 82.3 %collective-permute-done.13 = bf16[512,4416]{0,1:T(8,128)(2,1)} collective-permute-done((bf16[512,4416]{0,1:T(8,128)(2,1)}, bf16[512,4416]{0,1:T(8,128)(2,1)}, u32[]{:S(2)}, u32[]{:S(2)}) %collective-permute-start.13) | collective-permute-done | bytes 4522016 | tf_op jit(solution)/shard_map/ppermute | solution.py:525
  2074.9 80.2 %add_convert_fusion = bf16[4096,2048]{1,0:T(8,128)(2,1)} fusion(f32[4096,2048]{1,0:T(8,128)} %fusion, bf16[4096,4096]{1,0:T(8,128)(2,1)} %get-tuple-element.47, bf16[2048,8512]{0,1:T(8,128)(2,1)} %param.12), kind=kOutput, calls=%fused_computation.1 | convolution fusion | flops 68736253952 | bytes 100663296 | tf_op jit(solution)/shard_map/dot_general | solution.py:32
  2155.0 4.5 constant_dynamic-update-slice_fusion.2
  2159.5 4.5 constant_dynamic-update-slice_fusion.1
  2164.0 4.5 constant_dynamic-update-slice_fusion
  2171.0 4.7 constant_dynamic-update-slice_fusion.11
  2175.7 4.7 constant_dynamic-update-slice_fusion.10
  2180.4 4.7 constant_dynamic-update-slice_fusion.9
  (116 shorter events, 10.9 us)
Async XLA Ops:
  7.2 451.2 %all-gather.6.cloned.1.call-start = ((), (), s32[]{:S(2)}) async-start(), calls=%async_computation | async-start | bytes 10485760 | tf_op jit(solution)/shard_map/all_gather | solution.py:508
  97.7 104.3 %collective-permute-start = (bf16[16,4416]{1,0:T(8,128)(2,1)}, bf16[16,4416]{1,0:T(8,128)(2,1)}, u32[]{:S(2)}, u32[]{:S(2)}) collective-permute-start(bf16[16,4416]{1,0:T(8,128)(2,1)} %slice.112), channel_id=1, source_target_pairs={{0,1},{1,2},{2,3},{4,5},{5,6},{6,7}} | collective-permute-start | bytes 423944 | tf_op jit(solution)/shard_map/ppermute | solution.py:502
  103.2 77.6 %copy-start.15 = (s32[4096]{0:T(1024)S(1)}, s32[4096]{0:T(1024)}, u32[]{:S(2)}) copy-start(s32[4096]{0:T(1024)} %add_select_fusion.1) | copy-start | bytes 49156
  103.2 77.6 %copy-start.17 = (s32[256]{0:T(256)S(1)}, s32[256]{0:T(256)}, u32[]{:S(2)}) copy-start(s32[256]{0:T(256)} %and_select_fusion) | copy-start | bytes 3076
  103.2 77.6 %copy-start.19 = (pred[256]{0:T(512)(128)(4,1)S(1)}, pred[256]{0:T(512)(128)(4,1)}, u32[]{:S(2)}) copy-start(pred[256]{0:T(512)(128)(4,1)} %iota_compare_fusion.1) | copy-start | bytes 772
  186.8 13.7 copy-start.16
  186.8 13.7 copy-start.20
  186.8 15.2 copy-start.1
  200.5 51.5 %copy-start = (bf16[4096,64]{1,0:T(8,128)(2,1)}, bf16[4096,64]{1,0:T(8,128)(2,1)S(1)}, u32[]{:S(2)}) copy-start(bf16[4096,64]{1,0:T(8,128)(2,1)S(1)} %slice.113.dtr_ref) | copy-start | bytes 1572868
  201.9 50.1 %copy-start.2 = (f32[64]{0:T(128)S(1)}, f32[64]{0:T(128)}, u32[]{:S(2)}) copy-start(f32[64]{0:T(128)} %param.15) | copy-start | bytes 772
  201.9 50.1 %copy-start.3 = (f32[64]{0:T(128)S(1)}, f32[64]{0:T(128)}, u32[]{:S(2)}) copy-start(f32[64]{0:T(128)} %param.16) | copy-start | bytes 772
  367.8 1.3 copy-start.4
  369.1 1.4 copy-start.5
  370.6 578.0 %all-gather.8.cloned.1.call-start = ((), (), s32[]{:S(2)}) async-start(), calls=%async_computation.1 | async-start | bytes 10485760 | tf_op jit(solution)/shard_map/all_gather | solution.py:515
  370.8 86.9 %copy-start.22 = (pred[4,4]{0,1:T(4,128)(4,1)S(1)}, pred[4,4]{0,1:T(4,128)(4,1)}, u32[]{:S(2)}) copy-start(pred[4,4]{0,1:T(4,128)(4,1)} %iota_compare_fusion) | copy-start | bytes 52
  458.2 402.0 %copy-start.11 = (f32[4,4,4096]{2,0,1:T(4,128)}, f32[4,4,4096]{2,0,1:T(4,128)S(1)}, u32[]{:S(2)}) copy-start(f32[4,4,4096]{2,0,1:T(4,128)S(1)} %reshape.128) | copy-start | bytes 786436
  860.2 43.8 %copy-start.9 = (bf16[4096,512]{1,0:T(8,128)(2,1)S(1)}, bf16[4096,512]{1,0:T(8,128)(2,1)}, u32[]{:S(2)}) copy-start(bf16[4096,512]{1,0:T(8,128)(2,1)} %get-tuple-element.82) | copy-start | bytes 12582916
  904.0 52.1 %collective-permute-start.1 = (f32[4096,1024]{1,0:T(8,128)}, f32[4096,1024]{1,0:T(8,128)}, u32[]{:S(2)}, u32[]{:S(2)}) collective-permute-start(f32[4096,1024]{1,0:T(8,128)} %fusion.7), channel_id=1, source_target_pairs={{0,1},{1,0},{2,3},{3,2},{4,5},{5,4},{6,7},{7,6}} | collective-permute-start | bytes 50331656 | tf_op jit(solution)/shard_map/ppermute | solution.py:531
  904.0 43.5 %copy-start.21 = (f32[64]{0:T(128)S(1)}, f32[64]{0:T(128)}, u32[]{:S(2)}) copy-start(f32[64]{0:T(128)} %get-tuple-element.89) | copy-start | bytes 772
  904.0 49.2 %copy-start.7 = (f32[128,4096]{1,0:T(8,128)S(1)}, f32[128,4096]{1,0:T(8,128)}, u32[]{:S(2)}) copy-start(f32[128,4096]{1,0:T(8,128)} %multiply_reduce_fusion.1.hin_ref) | copy-start | bytes 6291460
  947.0 37.3 %collective-permute-start.2 = (f32[1024,4096]{1,0:T(8,128)}, f32[1024,4096]{1,0:T(8,128)}, u32[]{:S(2)}, u32[]{:S(2)}) collective-permute-start(f32[1024,4096]{1,0:T(8,128)} %fusion.12), channel_id=1, source_target_pairs={{0,1},{1,0},{2,3},{3,2},{4,5},{5,4},{6,7},{7,6}} | collective-permute-start | bytes 50331656 | tf_op jit(solution)/shard_map/ppermute | solution.py:533
  953.2 2.8 copy-start.8
  1013.4 366.8 %collective-permute-start.3 = (f32[4096,512]{1,0:T(8,128)}, f32[4096,512]{1,0:T(8,128)}, u32[]{:S(2)}, u32[]{:S(2)}) collective-permute-start(f32[4096,512]{1,0:T(8,128)} %slice_add_fusion.5), channel_id=1, source_target_pairs={{0,2},{1,3},{2,0},{3,1},{4,6},{5,7},{6,4},{7,5}} | collective-permute-start | bytes 25165832 | tf_op jit(solution)/shard_map/ppermute | solution.py:540
  1013.4 366.8 %collective-permute-start.4 = (f32[512,4096]{1,0:T(8,128)}, f32[512,4096]{1,0:T(8,128)}, u32[]{:S(2)}, u32[]{:S(2)}) collective-permute-start(f32[512,4096]{1,0:T(8,128)} %slice_add_fusion.4), channel_id=1, source_target_pairs={{0,2},{1,3},{2,0},{3,1},{4,6},{5,7},{6,4},{7,5}} | collective-permute-start | bytes 25165832 | tf_op jit(solution)/shard_map/ppermute | solution.py:541
  1380.1 135.0 %copy-start.10 = (bf16[4096,64]{1,0:T(8,128)(2,1)S(1)}, bf16[4096,64]{1,0:T(8,128)(2,1)}, u32[]{:S(2)}) copy-start(bf16[4096,64]{1,0:T(8,128)(2,1)} %get-tuple-element.63) | copy-start | bytes 1572868
  1511.1 3.2 collective-permute-start.5
  1516.3 49.3 %copy-start.14 = (f32[8,4096]{1,0:T(8,128)S(1)}, f32[8,4096]{1,0:T(8,128)}, u32[]{:S(2)}) copy-start(f32[8,4096]{1,0:T(8,128)} %get-tuple-element.69) | copy-start | bytes 393220
  1516.3 49.5 %copy-start.13 = (f32[8,4096]{1,0:T(8,128)S(1)}, f32[8,4096]{1,0:T(8,128)}, u32[]{:S(2)}) copy-start(f32[8,4096]{1,0:T(8,128)} %get-tuple-element.70) | copy-start | bytes 393220
  1516.3 49.6 %copy-start.18 = (f32[8,128]{1,0:T(8,128)S(1)}, f32[8,128]{1,0:T(8,128)}, u32[]{:S(2)}) copy-start(f32[8,128]{1,0:T(8,128)} %get-tuple-element.68) | copy-start | bytes 12292
  1562.9 41.2 %collective-permute-start.9 = (f32[1024,4416]{0,1:T(8,128)}, f32[1024,4416]{0,1:T(8,128)}, u32[]{:S(2)}, u32[]{:S(2)}) collective-permute-start(f32[1024,4416]{0,1:T(8,128)} %fusion.11), channel_id=1, source_target_pairs={{0,1},{1,0},{2,3},{3,2},{4,5},{5,4},{6,7},{7,6}} | collective-permute-start | bytes 54263816 | tf_op jit(solution)/shard_map/ppermute | solution.py:561
  1566.2 26.2 %collective-permute-start.10 = (f32[26048]{0:T(1024)S(1)}, f32[26048]{0:T(1024)S(1)}, u32[]{:S(2)}, u32[]{:S(2)}) collective-permute-start(f32[26048]{0:T(1024)S(1)} %concatenate.11), channel_id=1, source_target_pairs={{0,1},{1,0},{2,3},{3,2},{4,5},{5,4},{6,7},{7,6}} | collective-permute-start | bytes 312584 | tf_op jit(solution)/shard_map/ppermute | solution.py:557
  1592.4 11.0 collective-permute-start.11
  1601.5 93.4 %collective-permute-start.6 = (bf16[512,4096]{1,0:T(8,128)(2,1)}, bf16[512,4096]{1,0:T(8,128)(2,1)}, u32[]{:S(2)}, u32[]{:S(2)}) collective-permute-start(bf16[512,4096]{1,0:T(8,128)(2,1)} %add_convert_fusion.2), channel_id=1, source_target_pairs={{0,2},{1,3},{2,0},{3,1},{4,6},{5,7},{6,4},{7,5}} | collective-permute-start | bytes 12582920 | tf_op jit(solution)/shard_map/ppermute | solution.py:525
  1631.9 256.8 %collective-permute-start.12 = (f32[512,4416]{0,1:T(8,128)}, f32[512,4416]{0,1:T(8,128)}, u32[]{:S(2)}, u32[]{:S(2)}) collective-permute-start(f32[512,4416]{0,1:T(8,128)} %slice_add_fusion), channel_id=1, source_target_pairs={{0,2},{1,3},{2,0},{3,1},{4,6},{5,7},{6,4},{7,5}} | collective-permute-start | bytes 27131912 | tf_op jit(solution)/shard_map/ppermute | solution.py:564
  1638.5 90.1 %collective-permute-start.7 = (bf16[512,4096]{1,0:T(8,128)(2,1)}, bf16[512,4096]{1,0:T(8,128)(2,1)}, u32[]{:S(2)}, u32[]{:S(2)}) collective-permute-start(bf16[512,4096]{1,0:T(8,128)(2,1)} %add_convert_fusion.2), channel_id=1, source_target_pairs={{0,1},{1,0},{2,3},{3,2},{4,5},{5,4},{6,7},{7,6}} | collective-permute-start | bytes 12582920 | tf_op jit(solution)/shard_map/ppermute | solution.py:526
  1655.2 13.8 copy-start.6
  1655.2 336.9 %collective-permute-start.16 = (bf16[4096,512]{1,0:T(8,128)(2,1)}, bf16[4096,512]{1,0:T(8,128)(2,1)}, u32[]{:S(2)}, u32[]{:S(2)}) collective-permute-start(bf16[4096,512]{1,0:T(8,128)(2,1)} %get-tuple-element.79), channel_id=1, source_target_pairs={{0,2},{1,3},{2,0},{3,1},{4,6},{5,7},{6,4},{7,5}} | collective-permute-start | bytes 12582920 | tf_op jit(solution)/shard_map/ppermute | solution.py:525
  1657.2 502.3 %collective-permute-start.17 = (bf16[4096,512]{1,0:T(8,128)(2,1)}, bf16[4096,512]{1,0:T(8,128)(2,1)}, u32[]{:S(2)}, u32[]{:S(2)}) collective-permute-start(bf16[4096,512]{1,0:T(8,128)(2,1)} %get-tuple-element.79), channel_id=1, source_target_pairs={{0,1},{1,0},{2,3},{3,2},{4,5},{5,4},{6,7},{7,6}} | collective-permute-start | bytes 12582920 | tf_op jit(solution)/shard_map/ppermute | solution.py:526
  1695.0 49.1 %collective-permute-start.8 = (bf16[512,4096]{1,0:T(8,128)(2,1)}, bf16[512,4096]{1,0:T(8,128)(2,1)}, u32[]{:S(2)}, u32[]{:S(2)}) collective-permute-start(bf16[512,4096]{1,0:T(8,128)(2,1)} %collective-permute-done.6), channel_id=1, source_target_pairs={{0,1},{1,0},{2,3},{3,2},{4,5},{5,4},{6,7},{7,6}} | collective-permute-start | bytes 12582920 | tf_op jit(solution)/shard_map/ppermute | solution.py:527
  1902.7 172.2 %collective-permute-start.13 = (bf16[512,4416]{0,1:T(8,128)(2,1)}, bf16[512,4416]{0,1:T(8,128)(2,1)}, u32[]{:S(2)}, u32[]{:S(2)}) collective-permute-start(bf16[512,4416]{0,1:T(8,128)(2,1)} %get-tuple-element.81), channel_id=1, source_target_pairs={{0,2},{1,3},{2,0},{3,1},{4,6},{5,7},{6,4},{7,5}} | collective-permute-start | bytes 13565960 | tf_op jit(solution)/shard_map/ppermute | solution.py:525
  1992.1 171.9 %collective-permute-start.18 = (bf16[4096,512]{1,0:T(8,128)(2,1)}, bf16[4096,512]{1,0:T(8,128)(2,1)}, u32[]{:S(2)}, u32[]{:S(2)}) collective-permute-start(bf16[4096,512]{1,0:T(8,128)(2,1)} %collective-permute-done.16), channel_id=1, source_target_pairs={{0,1},{1,0},{2,3},{3,2},{4,5},{5,4},{6,7},{7,6}} | collective-permute-start | bytes 12582920 | tf_op jit(solution)/shard_map/ppermute | solution.py:527
  1992.1 183.6 %collective-permute-start.14 = (bf16[512,4416]{0,1:T(8,128)(2,1)}, bf16[512,4416]{0,1:T(8,128)(2,1)}, u32[]{:S(2)}, u32[]{:S(2)}) collective-permute-start(bf16[512,4416]{0,1:T(8,128)(2,1)} %get-tuple-element.81), channel_id=1, source_target_pairs={{0,1},{1,0},{2,3},{3,2},{4,5},{5,4},{6,7},{7,6}} | collective-permute-start | bytes 13565960 | tf_op jit(solution)/shard_map/ppermute | solution.py:526
  2074.9 105.5 %collective-permute-start.15 = (bf16[512,4416]{0,1:T(8,128)(2,1)}, bf16[512,4416]{0,1:T(8,128)(2,1)}, u32[]{:S(2)}, u32[]{:S(2)}) collective-permute-start(bf16[512,4416]{0,1:T(8,128)(2,1)} %collective-permute-done.13), channel_id=1, source_target_pairs={{0,1},{1,0},{2,3},{3,2},{4,5},{5,4},{6,7},{7,6}} | collective-permute-start | bytes 13565960 | tf_op jit(solution)/shard_map/ppermute | solution.py:527
  2155.0 13.5 copy-start.12
  2155.0 14.8 slice-start
Sparse Core Ops, SparseCore 0:
  370.7 57.3 all-gather.5
  860.3 56.4 all-gather.7

commit v2 on v1

v2 whole, which is shorter than its diff:
```python
import jax
import jax.numpy as jnp
from jax import lax
from jax.experimental import pallas as pl
from jax.experimental.pallas import tpu as pltpu
from jax.sharding import PartitionSpec as P

Q = 256
N = 128
H = 64
E = 4096
CD = E + 2 * N
PX = CD + H
KCONV = 4
EPS = 1e-5
LOG2E = 1.4426950408889634
F32 = jnp.float32
BF16 = jnp.bfloat16
HB = 128
R8 = 8
R16 = 16


def _dot(a, b):
    return lax.dot_general(a, b, (((1,), (0,)), ((), ())), preferred_element_type=F32)


def _tn(a, b):
    return lax.dot_general(a, b, (((0,), (0,)), ((), ())), preferred_element_type=F32)


def _nt(a, b):
    return lax.dot_general(a, b, (((1,), (1,)), ((), ())), preferred_element_type=F32)


def _twice(body, a, b):
    def step(j, _):
        body(2 * j, *a)
        body(2 * j + 1, *b)
        return 0

    lax.fori_loop(0, E // 512, step, 0)


def _lanes(j, w):
    return pl.ds(pl.multiple_of(j * w, w), w)


def _iota(shape, d):
    return lax.broadcasted_iota(jnp.int32, shape, d)


def _split3(v):
    hi = v.astype(BF16).astype(F32)
    mid = (v - hi).astype(BF16).astype(F32)
    lo = v - hi - mid
    return jnp.concatenate([hi, mid, lo, jnp.zeros_like(v)], 1).astype(BF16)


def _sum3(v):
    return v[:, :H] + v[:, H:2 * H] + v[:, 2 * H:3 * H]


def _split2(v):
    hi = v.astype(BF16)
    return hi, (v - hi.astype(F32)).astype(BF16)


def _softplus(v):
    return jnp.maximum(v, 0.0) + jnp.log1p(jnp.exp(-jnp.abs(v)))


def _const(shape):
    return pl.BlockSpec(shape, lambda i: (0,) * len(shape), pipeline_mode=pl.Buffered(1))


def _params(mb, **kw):
    return pltpu.CompilerParams(dimension_semantics=('arbitrary',), vmem_limit_bytes=mb * 1024 * 1024, **kw)


def _cost(flops, nbytes):
    return pl.CostEstimate(flops=int(flops), bytes_accessed=int(nbytes), transcendentals=0)


def _load_taps(x_ref, halo_ref, scr, r, h):
    hl = slice(h * N, h * N + N)
    at = pl.multiple_of(jnp.maximum(r * Q - R16, 0), R16)
    scr[0:R16, :] = jnp.where(r == 0, halo_ref[:, hl], x_ref[pl.ds(at, R16), hl]).astype(F32)
    scr[R16:, :] = x_ref[pl.ds(pl.multiple_of(r * Q, Q), Q), hl].astype(F32)


def _conv_fwd_kernel(x_ref, halo_ref, w_ref, b_ref, o_ref, *scrs):
    nr = x_ref.shape[0] // Q

    def body(r, _):
        for h, scr in enumerate(scrs):
            hl = slice(h * N, h * N + N)
            _load_taps(x_ref, halo_ref, scr, r, h)
            u = b_ref[:, hl] + sum(w_ref[k:k + 1, hl] * scr[R16 - k:R16 - k + Q, :] for k in range(KCONV))
            o_ref[pl.ds(pl.multiple_of(r * Q, Q), Q), hl] = (u * jax.nn.sigmoid(u)).astype(BF16)
        return 0

    lax.fori_loop(0, nr, body, 0)


def _conv_fwd(xb, halo, w, b, cw=Q):
    t = xb.shape[0]
    return pl.pallas_call(
        _conv_fwd_kernel,
        grid=(CD // cw,),
        in_specs=[pl.BlockSpec((t, cw), lambda i: (0, i)), pl.BlockSpec((R16, cw), lambda i: (0, i)),
                  pl.BlockSpec((KCONV, cw), lambda i: (0, i)), pl.BlockSpec((1, cw), lambda i: (0, i))],
        out_specs=pl.BlockSpec((t, cw), lambda i: (0, i)),
        out_shape=jax.ShapeDtypeStruct((t, CD), BF16),
        scratch_shapes=[pltpu.VMEM((Q + R16, N), F32)] * (cw // N),
        compiler_params=_params(40),
        cost_estimate=_cost(25e9, 4 * t * CD),
        name='conv_fwd',
    )(xb, halo, w, b)


def _conv_bwd_kernel(x_ref, halo_ref, d_ref, w_ref, b_ref, o_ref, gw_ref, gb_ref, tail_ref, *scrs):
    nr = x_ref.shape[0] // Q
    nh = x_ref.shape[1] // N
    xscr, dscr = scrs[:nh], scrs[nh:]
    gw_ref[...] = jnp.zeros_like(gw_ref)
    gb_ref[...] = jnp.zeros_like(gb_ref)
    for d in dscr:
        d[0:R8, :] = jnp.zeros((R8, N), F32)

    def fold(v):
        return jnp.sum(v.reshape(Q // R8, R8, N), 0)

    def body(k, _):
        r = nr - 1 - k
        rows = pl.ds(pl.multiple_of(r * Q, Q), Q)
        for h in range(nh):
            hl = slice(h * N, h * N + N)
            scr, d = xscr[h], dscr[h]
            _load_taps(x_ref, halo_ref, scr, r, h)
            u = b_ref[:, hl] + sum(w_ref[i:i + 1, hl] * scr[R16 - i:R16 - i + Q, :] for i in range(KCONV))
            sg = jax.nn.sigmoid(u)
            du = d_ref[rows, hl].astype(F32) * (sg * (1.0 + u * (1.0 - sg)))
            d[Q:, :] = d[0:R8, :]
            d[0:Q, :] = du
            gb_ref[:, hl] += fold(du)
            for i in range(KCONV):
                gw_ref[R8 * i:R8 * i + R8, hl] += fold(du * scr[R16 - i:R16 - i + Q, :])
            dx = sum(w_ref[i:i + 1, hl] * d[i:i + Q, :] for i in range(KCONV))
            o_ref[rows, hl] = dx.astype(BF16)

            @pl.when(k == 0)
            def _():
                tail_ref[:, hl] = dx[Q - R16:]

        return 0

    lax.fori_loop(0, nr, body, 0)


def _conv_bwd(xb, halo, dxc, w, b, cw=Q):
    t = xb.shape[0]
    col = lambda r: pl.BlockSpec((r, cw), lambda i: (0, i))
    return pl.pallas_call(
        _conv_bwd_kernel,
        grid=(CD // cw,),
        in_specs=[col(t), col(R16), col(t), col(KCONV), col(1)],
        out_specs=[col(t), col(R8 * KCONV), col(R8), col(R16)],
        out_shape=[jax.ShapeDtypeStruct((t, PX), BF16), jax.ShapeDtypeStruct((R8 * KCONV, CD), F32),
                   jax.ShapeDtypeStruct((R8, CD), F32), jax.ShapeDtypeStruct((R16, CD), F32)],
        scratch_shapes=[pltpu.VMEM((Q + R16, N), F32)] * (cw // N) + [pltpu.VMEM((Q + R8, N), F32)] * (cw // N),
        compiler_params=_params(40),
        cost_estimate=_cost(50e9, 6 * t * CD),
        name='conv_bwd',
    )(xb, halo, dxc, w, b)


def _state_kernel(xc_ref, dtr_ref, bias_ref, al_ref, e_ref, cd_ref, cdt_ref, c3_ref, d3_ref, ec3_ref, f3_ref, hst_ref, h_ref,
                  s_ref, fe_s):
    i = pl.program_id(0)

    @pl.when(i == 0)
    def _():
        h_ref[...] = jnp.zeros_like(h_ref)
        s_ref[...] = jnp.zeros_like(s_ref)

    dt = _softplus(dtr_ref[...].astype(F32) + bias_ref[...])
    a = -jnp.exp(al_ref[...]) * dt
    tri = (_iota((Q, Q), 0) >= _iota((Q, Q), 1)).astype(BF16)
    c = _sum3(_dot(tri, _split3(a)))
    s_ref[...] += jnp.broadcast_to(c[Q - 1:Q], s_ref.shape)
    c2 = c * LOG2E
    cd = jnp.concatenate([c2, dt], 1)
    cd_ref[...] = cd
    cdt_ref[...] = cd.T
    c3_ref[...] = _split3(c2)
    d3_ref[...] = _split3(dt)
    ec3 = _split3(jnp.exp2(c2))
    ec3_ref[...] = ec3
    f3 = _split3(dt * jnp.exp2(c2[Q - 1:Q] - c2))
    f3_ref[...] = f3
    fe_s[0:Q, :] = f3
    fe_s[Q:, :] = ec3[Q - R16:]
    bt = xc_ref[:, E:E + N].astype(F32).T.astype(BF16)

    def body(j, _):
        L = _lanes(j, 512)
        fe = _dot(fe_s[...], e_ref[:, L])
        xw = (xc_ref[:, L].astype(F32) * fe[:Q]).astype(BF16)
        st = _dot(bt, xw)
        h = h_ref[:, L]
        hst_ref[:, L] = h
        h_ref[:, L] = h * fe[Q + 15:Q + R16] + st
        return 0

    lax.fori_loop(0, E // 512, body, 0)


def _states(xc, dtr, bias, al, e64):
    t = xc.shape[0]
    nc = t // Q
    row = lambda w: pl.BlockSpec((Q, w), lambda i: (i, 0))
    return pl.pallas_call(
        _state_kernel,
        grid=(nc,),
        in_specs=[row(CD), row(H), _const((1, H)), _const((1, H)), _const((Q, E))],
        out_specs=[row(2 * H), pl.BlockSpec((None, 2 * H, Q), lambda i: (i, 0, 0))] + [row(Q)] * 4 + [
                   pl.BlockSpec((None, N, E), lambda i: (i, 0, 0)), pl.BlockSpec((N, E), lambda i: (0, 0)),
                   pl.BlockSpec((R8, H), lambda i: (0, 0))],
        out_shape=[jax.ShapeDtypeStruct((t, 2 * H), F32), jax.ShapeDtypeStruct((nc, 2 * H, Q), F32)]
                  + [jax.ShapeDtypeStruct((t, Q), BF16)] * 4 + [
                   jax.ShapeDtypeStruct((nc, N, E), F32), jax.ShapeDtypeStruct((N, E), F32),
                   jax.ShapeDtypeStruct((R8, H), F32)],
        scratch_shapes=[pltpu.VMEM((Q + R16, Q), BF16)],
        compiler_params=_params(48),
        cost_estimate=_cost(25e9, 70e6),
        name='states',
    )(xc, dtr, bias, al, e64)


def _fwd_kernel(xc_ref, c3_ref, ec3_ref, cdt_ref, hst_ref, hin_ref, z_ref, dyn_ref, d_ref, nw_ref, e_ref, e2_ref,
                yn_ref, dz_ref, dy_ref, hs_ref, dh_ref, gl_ref, row_ref, dnw_ref, dd_ref,
                y_s, sc_a, sc_b, xm_a, xm_b, cb_s, ece, acc1, acc2, p_a, p_b, q_a, q_b):
    i = pl.program_id(0)

    @pl.when(i == 0)
    def _():
        for b in (sc_a, sc_b):
            b[...] = jnp.zeros_like(b)
        ece[...] = jnp.ones_like(ece)
        gl_ref[...] = jnp.zeros_like(gl_ref)
        dnw_ref[...] = jnp.zeros_like(dnw_ref)
        dd_ref[...] = jnp.zeros_like(dd_ref)

    bm = xc_ref[:, E:E + N]
    cm = xc_ref[:, E + N:]
    ct = cm.astype(F32).T.astype(BF16)
    causal = _iota((Q, Q), 0) >= _iota((Q, Q), 1)
    cb_s[...] = jnp.where(causal, _nt(cm, bm), 0.0)
    acc1[...] = jnp.zeros_like(acc1)
    acc2[...] = jnp.zeros_like(acc2)
    head = _iota((1, Q), 1) // H

    def quad(j, sc_s, xm_s):
        L = _lanes(j, Q)
        ej = e_ref[:, L]
        xq = xc_ref[:, L]
        ccol = _dot(c3_ref[...], e2_ref[:, _lanes(j, 512)])
        h = hst_ref[:, L] + ece[0:1, L] * hin_ref[:, L]
        hs_ref[:, L] = h
        yi = _dot(cm, h.astype(BF16)) * _dot(ec3_ref[...], ej)
        for k in range(4):
            crow = cdt_ref[pl.ds(4 * j + k, 1), :]
            drow = cdt_ref[pl.ds(H + 4 * j + k, 1), :]
            cc = ccol[:, k * N:k * N + N]
            for (a, b) in ((0, 0), (1, 0), (1, 1)):
                ra, rb = slice(a * HB, a * HB + HB), slice(b * HB, b * HB + HB)
                seg = jnp.minimum(cc[ra] - crow[:, rb], 0.0)
                w = jnp.exp2(seg) * drow[:, rb]
                sc_s[ra, k * Q + b * HB:k * Q + b * HB + HB] = (cb_s[ra, rb] * w).astype(BF16)
            xm_s[k * Q:k * Q + Q, :] = jnp.where(head == k, xq, jnp.zeros_like(xq))
        y = yi + _dot(sc_s[...], xm_s[...])
        y_s[:, L] = y
        z = z_ref[:, L].astype(F32)
        g = (y + d_ref[:, L] * xq.astype(F32)) * (z * jax.nn.sigmoid(z))
        gg = g * g
        gd = g * (dyn_ref[:, L].astype(F32) * nw_ref[:, L])
        acc1[...] += gg[:, :N] + gg[:, N:]
        acc2[...] += gd[:, :N] + gd[:, N:]

    _twice(quad, (sc_a, xm_a), (sc_b, xm_b))
    r = lax.rsqrt(jnp.sum(acc1[...], 1, keepdims=True) / E + EPS)
    m = jnp.sum(acc2[...], 1, keepdims=True) / E * (r * r * r)
    acc1[...] = jnp.broadcast_to(r, acc1.shape)
    acc2[...] = jnp.broadcast_to(m, acc2.shape)
    row_ref[...] = jnp.zeros_like(row_ref)
    RB = H

    def gate(j, p_s, q_s):
        L = _lanes(j, Q)
        ej = e_ref[:, L]
        ecq = _dot(ec3_ref[...], ej)
        nw = nw_ref[:, L]
        dk = d_ref[:, L]
        dnw = dd = None
        for k in range(Q // RB):
            R = slice(k * RB, k * RB + RB)
            x = xc_ref[R, L].astype(F32)
            ys = y_s[R, L]
            y = ys + dk * x
            z = z_ref[R, L].astype(F32)
            sg = jax.nn.sigmoid(z)
            sz = z * sg
            g = y * sz
            rb = jnp.concatenate([acc1[R, :], acc1[R, :]], 1)
            mb = jnp.concatenate([acc2[R, :], acc2[R, :]], 1)
            gr = g * rb
            dn = dyn_ref[R, L].astype(F32)
            yn_ref[R, L] = (gr * nw).astype(BF16)
            a = jnp.sum((dn * gr).reshape(RB // R8, R8, Q), 0)
            dnw = a if dnw is None else dnw + a
            dg = rb * (dn * nw) - g * mb
            dy = dg * sz
            dz_ref[R, L] = (dg * y * (sg + sz * (1.0 - sg))).astype(BF16)
            dy_ref[R, L] = dy
            a = jnp.sum((dy * x).reshape(RB // R8, R8, Q), 0)
            dd = a if dd is None else dd + a
            hi, lo = _split2(dy.astype(BF16).astype(F32) * ys)
            p_s[R, :] = hi
            p_s[Q + k * RB:Q + k * RB + RB, :] = lo
            q_s[R, :] = (ecq[R] * dy).astype(BF16)
        dnw_ref[:, L] += dnw
        dd_ref[:, L] += dd
        pr = _nt(p_s[...], e_ref[0:2 * H, L])
        row_ref[...] += pr[:Q] + pr[Q:]
        dh = _dot(ct, q_s[...]).astype(BF16)
        dh_ref[:, L] = dh
        gl_ref[:, L] += ece[0:1, L] * dh.astype(F32)
        ece[:, L] = ece[:, L] * ecq[Q - 1:Q]

    _twice(gate, (p_a, q_a), (p_b, q_b))


def _fwd(xc, c3, ec3, cdt, hst, hin, z, dyn, dx, nw, e64, e128):
    t = xc.shape[0]
    nc = t // Q
    row = lambda w: pl.BlockSpec((Q, w), lambda i: (i, 0))
    blk = lambda a, b: pl.BlockSpec((None, a, b), lambda i: (i, 0, 0))
    fix = lambda a, b: pl.BlockSpec((a, b), lambda i: (0, 0))
    return pl.pallas_call(
        _fwd_kernel,
        grid=(nc,),
        in_specs=[row(CD), row(Q), row(Q), blk(2 * H, Q), blk(N, E), _const((N, E)), row(E), row(E), _const((1, E)),
                  _const((1, E)), _const((Q, E)), _const((Q, 2 * E))],
        out_specs=[row(E), row(E), row(E), blk(N, E), blk(N, E), fix(N, E), row(2 * H), fix(R8, E), fix(R8, E)],
        out_shape=[jax.ShapeDtypeStruct((t, E), BF16), jax.ShapeDtypeStruct((t, E), BF16),
                   jax.ShapeDtypeStruct((t, E), F32), jax.ShapeDtypeStruct((nc, N, E), F32),
                   jax.ShapeDtypeStruct((nc, N, E), BF16), jax.ShapeDtypeStruct((N, E), F32),
                   jax.ShapeDtypeStruct((t, 2 * H), F32), jax.ShapeDtypeStruct((R8, E), F32),
                   jax.ShapeDtypeStruct((R8, E), F32)],
        scratch_shapes=[pltpu.VMEM((Q, E), F32)] + [pltpu.VMEM((Q, 4 * Q), BF16)] * 2 + [pltpu.VMEM((4 * Q, Q), BF16)] * 2 + [
                        pltpu.VMEM((Q, Q), F32), pltpu.VMEM((R8, E), F32), pltpu.VMEM((Q, N), F32),
                        pltpu.VMEM((Q, N), F32)] + [pltpu.VMEM((2 * Q, Q), BF16)] * 2 + [pltpu.VMEM((Q, Q), BF16)] * 2,
        compiler_params=_params(60),
        cost_estimate=_cost(150e9, 270e6),
        name='ssd_fwd_gate',
    )(xc, c3, ec3, cdt, hst, hin, z, dyn, dx, nw, e64, e128)


def _bwd_kernel(xc_ref, cd_ref, c3_ref, d3_ref, ec3_ref, f3_ref, cdt_ref, hs_ref, dh_ref, gin_ref, dae_ref, dy_ref, row_ref, d_ref, dtr_ref, bias_ref,
                al_ref, e_ref, e2_ref,
                dxc_ref, ddtr_ref, red_ref,
                g_s, cb_s, dcb_s, dae_s, col_s, db_s, dc_s, sc_a, sc_b, xm_a, xm_b, dm_a, dm_b, w_a, w_b, p_a, p_b):
    i = pl.program_id(0)

    @pl.when(i == 0)
    def _():
        for b in (sc_a, sc_b):
            b[...] = jnp.zeros_like(b)
        g_s[...] = gin_ref[...]
        dae_s[...] = dae_ref[...]
        red_ref[...] = jnp.zeros_like(red_ref)

    dt = cd_ref[:, H:]
    bm = xc_ref[:, E:E + N]
    cm = xc_ref[:, E + N:]
    causal = _iota((Q, Q), 0) <= _iota((Q, Q), 1)
    cb_s[...] = jnp.where(causal, _nt(bm, cm), 0.0)
    dcb_s[...] = jnp.zeros_like(dcb_s)
    col_s[...] = jnp.zeros_like(col_s)
    db_s[...] = jnp.zeros_like(db_s)
    dc_s[...] = jnp.zeros_like(dc_s)
    head = _iota((1, Q), 1) // H
    dae_h = dae_s[0:1, :H]
    dae_s[...] = jnp.zeros_like(dae_s)

    def quad(j, sc_s, xm_s, dm_s, w_s, p_s):
        L = _lanes(j, Q)
        ej = e_ref[:, L]
        xq = xc_ref[:, L]
        dy = dy_ref[:, L]
        dyb = dy.astype(BF16)
        for k in range(4):
            sel = head == k
            xm_s[k * Q:k * Q + Q, :] = jnp.where(sel, xq, jnp.zeros_like(xq))
            dm_s[k * Q:k * Q + Q, :] = jnp.where(sel, dyb, jnp.zeros_like(dyb))
        e2j = e2_ref[:, _lanes(j, 512)]
        ccol = _dot(c3_ref[...], e2j)
        dcol = _dot(d3_ref[...], e2j)
        w_s[...] = _nt(xm_s[...], dyb)
        for k in range(4):
            crow = cdt_ref[pl.ds(4 * j + k, 1), :]
            cc = ccol[:, k * N:k * N + N]
            dc = dcol[:, k * N:k * N + N]
            for (a, b) in ((0, 0), (0, 1), (1, 1)):
                ra, rb = slice(a * HB, a * HB + HB), slice(b * HB, b * HB + HB)
                seg = jnp.minimum(crow[:, rb] - cc[ra], 0.0)
                w = jnp.exp2(seg) * dc[ra]
                sc_s[ra, k * Q + b * HB:k * Q + b * HB + HB] = (cb_s[ra, rb] * w).astype(BF16)
                ds = w_s[k * Q + a * HB:k * Q + a * HB + HB, rb].astype(BF16).astype(F32)
                dcb_s[ra, rb] += ds * w
        dxs = _dot(sc_s[...], dm_s[...])
        fq = _dot(f3_ref[...], ej)
        g = g_s[:, L]
        gb = g.astype(BF16)
        x = xq.astype(F32)
        dxw = _dot(bm, gb).astype(BF16).astype(F32)
        dxs = dxs + fq * dxw
        db_s[...] += _nt((x * fq).astype(BF16), gb)
        ecq = _dot(ec3_ref[...], ej)
        hs = hs_ref[:, L]
        dc_s[...] += _nt((ecq * dy).astype(BF16), hs.astype(BF16))
        hi, lo = _split2(x * dxs)
        p_s[0:Q, :] = hi
        p_s[Q:2 * Q, :] = lo
        dxc_ref[:, L] = (dxs + d_ref[:, L] * dy).astype(BF16)
        gn = g * ecq[Q - 1:Q] + dh_ref[:, L].astype(F32)
        g_s[:, L] = gn
        dr = jnp.broadcast_to(jnp.sum(gn * hs, 0, keepdims=True), (R16, Q))
        hi, lo = _split2(dr)
        p_s[2 * Q:2 * Q + R16, :] = hi
        p_s[2 * Q + R16:2 * Q + 32, :] = lo
        p_s[2 * Q + 32:, :] = (dr - hi.astype(F32) - lo.astype(F32)).astype(BF16)
        pr = _nt(p_s[...], e_ref[0:2 * H, L])
        col_s[...] += pr[:Q] + pr[Q:2 * Q]
        dae_s[...] += pr[2 * Q:2 * Q + R8] + pr[2 * Q + R16:2 * Q + 24] + pr[2 * Q + 32:2 * Q + 40]

    _twice(quad, (sc_a, xm_a, dm_a, w_a, p_a), (sc_b, xm_b, dm_b, w_b, p_b))
    dcb = jnp.where(causal, dcb_s[...], 0.0)
    dxc_ref[:, E:E + N] = (db_s[...] + _dot(dcb.astype(BF16), cm)).astype(BF16)
    dxc_ref[:, E + N:] = (dc_s[...] + _dot(dcb.T.astype(BF16), bm)).astype(BF16)

    col = col_s[:, :H]
    dcs = row_ref[:, :H] - col
    dcs = dcs + jnp.where(_iota((Q, H), 0) == Q - 1, dae_h, 0.0)
    da = _sum3(_dot(causal.astype(BF16), _split3(dcs)))
    na = -jnp.exp(al_ref[...])
    ddt = jnp.where(dt > 0.0, col / jnp.where(dt > 0.0, dt, 1.0), 0.0) + da * na
    ddtr = ddt * jax.nn.sigmoid(dtr_ref[...].astype(F32) + bias_ref[...])
    ddtr_ref[...] = ddtr.astype(BF16)
    both = jnp.concatenate([ddtr, da * (na * dt)], 1)
    red_ref[...] += jnp.sum(both.reshape(Q // R8, R8, 2 * H), 0)


def _bwd(xc, cd, c3, d3, ec3, f3, cdt, hs, dh, gin, dae, dy, row, dx, dtr, bias, al, e64, e128):
    t = xc.shape[0]
    nc = t // Q
    rows = lambda w: pl.BlockSpec((Q, w), lambda i: (nc - 1 - i, 0))
    blk = lambda a, b: pl.BlockSpec((None, a, b), lambda i: (nc - 1 - i, 0, 0))
    fix = lambda a, b: pl.BlockSpec((a, b), lambda i: (0, 0))
    return pl.pallas_call(
        _bwd_kernel,
        grid=(nc,),
        in_specs=[rows(CD), rows(2 * H)] + [rows(Q)] * 4 + [blk(2 * H, Q), blk(N, E), blk(N, E), _const((N, E)), _const((R8, 2 * H)), rows(E),
                  rows(2 * H), _const((1, E)), rows(H), _const((1, H)), _const((1, H)), _const((Q, E)),
                  _const((Q, 2 * E))],
        out_specs=[rows(CD), rows(H), fix(R8, 2 * H)],
        out_shape=[jax.ShapeDtypeStruct((t, CD), BF16), jax.ShapeDtypeStruct((t, H), BF16),
                   jax.ShapeDtypeStruct((R8, 2 * H), F32)],
        scratch_shapes=[pltpu.VMEM((N, E), F32), pltpu.VMEM((Q, Q), F32), pltpu.VMEM((Q, Q), F32), pltpu.VMEM((R8, 2 * H), F32),
                        pltpu.VMEM((Q, 2 * H), F32), pltpu.VMEM((Q, N), F32), pltpu.VMEM((Q, N), F32)]
                       + [pltpu.VMEM((Q, 4 * Q), BF16)] * 2 + [pltpu.VMEM((4 * Q, Q), BF16)] * 4
                       + [pltpu.VMEM((4 * Q, Q), F32)] * 2 + [pltpu.VMEM((2 * Q + 48, Q), BF16)] * 2,
        compiler_params=_params(60),
        cost_estimate=_cost(150e9, 220e6),
        name='ssd_bwd',
    )(xc, cd, c3, d3, ec3, f3, cdt, hs, dh, gin, dae, dy, row, dx, dtr, bias, al, e64, e128)


def _blank(shape):
    return pl.pallas_call(lambda o_ref: None, out_shape=jax.ShapeDtypeStruct(shape, BF16),
                          out_specs=pl.BlockSpec(memory_space=pl.ANY), name='blank')()


def _prefix(s):
    k = s.shape[0]
    cs = jnp.cumsum(s, 0)
    diff = (cs - s)[:, None] - cs[None, :]
    m = (jnp.arange(k)[:, None] > jnp.arange(k)[None, :]).reshape((k, k) + (1,) * (s.ndim - 1))
    return jnp.where(m, jnp.exp(jnp.where(m, diff, 0.0)), 0.0)


def _wide(v):
    return jnp.repeat(v, E // H, axis=-1)


def solution(mesh):
    nseq = mesh.shape['seq']
    fwd = [(i, i + 1) for i in range(nseq - 1)]
    bwd = [(i + 1, i) for i in range(nseq - 1)]
    core = [(i, i ^ 1) for i in range(nseq)]
    chip = [(i, i ^ 2) for i in range(nseq)]

    def layer(x, dout, W_in, conv_w, conv_b, dt_bias, A_log, D_skip, norm_w, W_out):
        t, dm = x.shape
        idx = lax.axis_index('seq')
        c, k = idx % 2, idx // 2
        rows = jnp.arange(Q)
        lane = jnp.arange(2 * E)
        e128 = ((rows[:, None] % H == lane[None, :] // N) & (rows[:, None] < 3 * H)).astype(BF16)
        e64 = ((rows[:, None] % H == lane[None, :E] // H) & (rows[:, None] < 3 * H)).astype(BF16)
        bias, al = dt_bias[None], A_log[None]
        dwide = _wide(D_skip)[None]
        Wz, Wx = W_in[:, :E], W_in[:, E:]

        xb = jnp.dot(x, Wx, preferred_element_type=F32).astype(BF16)
        halo = lax.ppermute(xb[t - R16:], 'seq', fwd)
        dtr = xb[:, CD:]
        xc = _conv_fwd(xb, halo, conv_w, conv_b[None])
        cd, cdt, c3, d3, ec3, f3, hst, h_loc, s8 = _states(xc, dtr, bias, al, e64)
        s = s8[0]
        s_all = lax.all_gather(s, 'seq')
        h_all = lax.all_gather(h_loc, 'seq')
        wd = _wide(_prefix(s_all))
        h_in = jnp.sum(wd[idx][:, None, :] * h_all, 0)
        h_fin = h_loc + _wide(jnp.exp(s))[None] * h_in
        z = jnp.dot(x, Wz, preferred_element_type=F32).astype(BF16)
        dyn = _nt(dout, W_out).astype(BF16)
        yn, dz, dy, hs, dh, g_loc, row, dnw8, dd8 = _fwd(xc, c3, ec3, cdt, hst, h_in, z, dyn, dwide, norm_w[None],
                                                              e64, e128)
        g_all = lax.all_gather(g_loc, 'seq')

        def quarters(a):
            w = a.shape[1] // 4
            cut = lambda cc, kk: lax.dynamic_slice_in_dim(a, (2 * cc + kk) * w, w, 1)
            return (jnp.concatenate([cut(1 - c, 1 - k), cut(1 - c, k)], 1), cut(c, 1 - k), cut(c, k))

        xs, ds = quarters(x), quarters(dout)

        def spread(mine):
            other = lax.ppermute(mine, 'seq', chip)
            mine_p = lax.ppermute(mine, 'seq', core)
            other_p = lax.ppermute(other, 'seq', core)
            return [(2 * c + k, mine), (2 * c + 1 - k, other), (2 - 2 * c + k, mine_p), (3 - 2 * c - k, other_p)]

        w4 = dm // 4
        sO = _tn(yn, ds[0])
        rO = lax.ppermute(sO, 'seq', core)
        sZ = _tn(dz, xs[0])
        rZ = lax.ppermute(sZ, 'seq', core)
        dh_fin = jnp.sum(wd[:, idx][:, None, :] * g_all, 0)
        dae = jnp.sum(jnp.sum(dh_fin * h_fin, 0).reshape(H, E // H), 1)
        dae = jnp.broadcast_to(jnp.concatenate([dae, dae])[None], (R8, 2 * H))
        fO = _tn(yn, ds[1]) + rO[:, :w4]
        gO = lax.ppermute(fO, 'seq', chip)
        fZ = _tn(dz, xs[1]) + rZ[:, :w4]
        gZ = lax.ppermute(fZ, 'seq', chip)
        dxc, ddtr, red = _bwd(xc, cd, c3, d3, ec3, f3, cdt, hs, dh, dh_fin, dae, dy, row, dwide, dtr, bias, al, e64, e128)
        oO = _tn(yn, ds[2]) + rO[:, w4:]
        oZ = _tn(dz, xs[2]) + rZ[:, w4:]
        xe = jnp.concatenate([halo[13:, :CD], xb[:R8, :CD]], 0).astype(F32)
        u = conv_b + sum(conv_w[j] * xe[3 - j:11 - j] for j in range(KCONV))
        sg = jax.nn.sigmoid(u)
        nxt = lax.ppermute(dxc[:R8].astype(F32) * (sg * (1.0 + u * (1.0 - sg))), 'seq', bwd)
        oO, oZ, dxc, gO, nxt = lax.optimization_barrier((oO, oZ, dxc, gO, nxt))
        pO = spread((oO + gO).astype(BF16))
        pZ = spread((oZ + gZ).astype(BF16))
        dxb, gw8, gb8, tail = _conv_bwd(xb, halo, dxc, conv_w, conv_b[None])
        fix = sum(conv_w[j] * jnp.pad(nxt[:j], ((R16 - j, 0), (0, 0))) for j in range(1, KCONV))
        dxb = lax.dynamic_update_slice(dxb, (tail + fix).astype(BF16), (t - R16, 0))
        dxb = lax.dynamic_update_slice(dxb, ddtr, (0, CD))

        dcw = jnp.sum(gw8.reshape(KCONV, R8, CD), 1)
        small = jnp.concatenate([dcw.reshape(-1), jnp.sum(gb8, 0), jnp.sum(red, 0), jnp.sum(dd8, 0).reshape(H, E // H).sum(1),
                                 jnp.sum(dnw8, 0)])
        small = small + lax.ppermute(small, 'seq', core)

        sX = _tn(dxb, xs[0])
        sX, small = lax.optimization_barrier((sX, small))
        rX = lax.ppermute(sX, 'seq', core)
        small = small + lax.ppermute(small, 'seq', chip)
        fX = _tn(dxb, xs[1]) + rX[:, :w4]
        gX = lax.ppermute(fX, 'seq', chip)
        oX = _tn(dxb, xs[2]) + rX[:, w4:]
        dx0 = _nt(dz, Wz)
        dx = (dx0 + _nt(dxb, Wx)).astype(BF16)
        gX, oX, dx = lax.optimization_barrier((gX, oX, dx))
        mX, pO, pZ = lax.optimization_barrier(((oX + gX).astype(BF16), [p for _, p in pO], [p for _, p in pZ]))
        pX = [p for _, p in spread(mX)]
        spots = (2 * c + k, 2 * c + 1 - k, 2 - 2 * c + k, 3 - 2 * c - k)

        def place(out, pieces, row=0):
            for pos, p in zip(spots, pieces):
                out = lax.dynamic_update_slice(out, p, (jnp.int32(row), pos * w4))
            return out

        dW_out = place(_blank((E, dm)), pO)
        dW_in = place(_blank((E + PX, dm)), pZ)
        dW_in = place(dW_in, pX, E).T
        cuts = []
        for n in (KCONV * CD, CD, H, H, H, E):
            cuts.append(small[:n])
            small = small[n:]
        dcw, dcb, ddtb, dal, dD, dnw = cuts
        dcw = dcw.reshape(KCONV, CD)
        return dx, dW_in, dcw, dcb, ddtb, dal, dD, dnw, dW_out

    xs = P(('data', 'seq'), None)
    return jax.shard_map(layer, mesh=mesh, in_specs=(xs, xs) + (P(),) * R8,
                         out_specs=(xs, P('data', None), P('data', None), P('data'), P('data'), P('data'),
                                    P('data'), P('data'), P('data', None)),
                         check_vma=False)
```

time: 2200 us -> 1870 us (0.85)
  Pallas kernels: 1000 us -> 764 us
  waiting for transfers between devices: 268 us -> 208 us
  local copies, waits for them, and re-layouts: 113 us -> 77.4 us
    pallas_call x2 -> x4, Pallas kernels: 704 us -> 548 us  [the longest x1 292 us: _fwd(): pl.pallas_call(_fwd_kernel, grid=(nc,), in_specs=[row(CD), row(Q), row(Q)...]
    ppermute x3, waiting for transfers between devices: 106 us -> 0.01 us  [spread(): other = lax.ppermute(mine, 'seq', chip)]
    pallas_call x1, Pallas kernels: 116 us -> 66.7 us  [_states(): pl.pallas_call(_state_kernel, grid=(nc,), in_specs=[row(CD), row(H), _con...]
    ppermute x10, waiting for transfers between devices: 162 us -> 203 us  [the longest x1 99.7 us: layer(): small = small + lax.ppermute(small, 'seq', chip)]
    dynamic_update_slice x3 -> x1, other arithmetic: 25.3 us -> 0.77 us  [layer(): dxb = lax.dynamic_update_slice(dxb, (tail + fix).astype(BF16), (t - R16, 0))]
    pallas_call x1, Pallas kernels: 131 us -> 107 us  [_conv_bwd(): pl.pallas_call(_conv_bwd_kernel, grid=(CD // cw,), in_specs=[col(t), col(...]
    dynamic_update_slice x11 -> x13, local copies, waits for them, and re-layouts: 44.4 us -> 49 us  [the longest x12 47.9 us: place(): out = lax.dynamic_update_slice(out, p, (jnp.int32(row), pos * w4))]
  transfers between devices with their start and end apart: 21 -> 21, of which waited for: 5 -> 4; matrix products, arithmetic and copies ran while one was open for 32% -> 37% of each run, Pallas kernels for 14% -> 20%
where the time goes in v2:
time: 1870 us; the launch traced here: 1860 us
  Pallas kernels  764 us (41%)
  matrix products  719 us (38%)
  waiting for transfers between devices  208 us (11%)
  local copies, waits for them, and re-layouts  77.4 us (4%)
  other arithmetic  55.7 us (3%)
    dot_general x9, matrix products, _tn(): lax.dot_general(a, b, (((0,), (0,)), ((), ())), preferred_element_type=F32)  307 us
    pallas_call x1, Pallas kernels, _fwd(): pl.pallas_call(_fwd_kernel, grid=(nc,), in_specs=[row(CD), row(Q), row(Q)...  292 us
    pallas_call x1, Pallas kernels, _bwd(): pl.pallas_call(_bwd_kernel, grid=(nc,), in_specs=[rows(CD), rows(2 * H)]...  256 us
    dot_general x3, matrix products, _nt(): lax.dot_general(a, b, (((1,), (1,)), ((), ())), preferred_element_type=F32)  246 us
    pallas_call x1, Pallas kernels, _conv_bwd(): pl.pallas_call(_conv_bwd_kernel, grid=(CD // cw,), in_specs=[col(t), col(...  107 us
    ppermute x1, waiting for transfers between devices, layer(): small = small + lax.ppermute(small, 'seq', chip)  99.7 us
    dot_general x1, matrix products, layer(): xb = jnp.dot(x, Wx, preferred_element_type=F32).astype(BF16)  88.9 us
    ppermute x1, waiting for transfers between devices, layer(): gX = lax.ppermute(fX, 'seq', chip)  87 us
  transfers between devices with their start and end apart: 21, of which 4 were waited for; matrix products, arithmetic and copies ran while one was open for 37% of the time, Pallas kernels for 20%

profile of v2, /device:TPU:0, one launch (start us, length us, event | category | flops | bytes accessed | tf_op | source)
XLA Modules:
  0.0 1860.4 jit_solution(8244367590023300083)
XLA Ops:
  7.2 88.9 %convolution_convert_fusion.x_ref = bf16[4096,4416]{1,0:T(8,128)(2,1)} fusion(bf16[4096,2048]{1,0:T(8,128)(2,1)} %param.10, bf16[2048,8512]{0,1:T(8,128)(2,1)} %param.12), kind=kOutput, calls=%fused_computation | convolution fusion | flops 74106273792 | bytes 71041024 | tf_op jit(solution)/shard_map/dot_general | solution.py:526
  96.1 1.6 slice.147
  97.7 3.6 collective-permute-start
  103.6 77.5 %convolution_convert_fusion.2.z_ref = bf16[4096,4096]{1,0:T(8,128)(2,1)} fusion(bf16[4096,2048]{1,0:T(8,128)(2,1)} %param.10, bf16[2048,8512]{0,1:T(8,128)(2,1)} %param.12), kind=kOutput, calls=%fused_computation.3 | convolution fusion | flops 68736253952 | bytes 67108864 | tf_op jit(solution)/shard_map/dot_general | solution.py:537
  181.1 2.3 and_convert_fusion.1.e_ref
  183.5 3.7 and_convert_fusion.e2_ref
  187.2 12.3 constant_dynamic-slice_fusion.1
  199.4 1.3 slice.148.dtr_ref
  200.9 0.8 broadcast_in_dim_reshape.4.d_ref
  202.2 41.7 %conv_fwd.1.xc_ref = bf16[4096,4352]{1,0:T(8,128)(2,1)} custom-call(bf16[4096,4416]{1,0:T(8,128)(2,1)} %convolution_convert_fusion.x_ref, bf16[16,4416]{1,0:T(8,128)(2,1)} %collective-permute-done.halo_ref, f32[4,4352]{1,0:T(4,128)S(1)} %copy-done.1, f32[1,4352]{1,0:T(1,128)S(1)} %broadcast_in_dim.57.b_ref), custom_call_target="tpu_custom_call" | custom-call | flops 24999999488 | bytes 71303168 | tf_op jit(solution)/shard_map/conv_fwd/pallas_call | solution.py:108
  243.9 66.7 %states.1 = (f32[4096,128]{1,0:T(8,128)S(1)}, f32[16,128,256]{2,1,0:T(8,128)S(1)}, bf16[4096,256]{1,0:T(8,128)(2,1)}, bf16[4096,256]{1,0:T(8,128)(2,1)}, bf16[40...) custom-call(bf16[4096,4352]{1,0:T(8,128)(2,1)} %conv_fwd.1.xc_ref, ...), custom_call_target="tpu_custom_call" | custom-call | flops 24999999488 | bytes 70000000 | tf_op jit(solution)/shard_map/states/pallas_call | solution.py:223
  310.6 1.3 copy-done.4
  311.9 1.4 copy-done.5
  313.8 77.7 %convolution_convert_fusion.1.dyn_ref = bf16[4096,4096]{1,0:T(8,128)(2,1)} fusion(bf16[4096,2048]{1,0:T(8,128)(2,1)} %param.11, bf16[4096,2048]{1,0:T(8,128)(2,1)} %param.19), kind=kOutput, calls=%fused_computation.2 | convolution fusion | flops 68736253952 | bytes 67108864 | tf_op jit(solution)/shard_map/dot_general | solution.py:33
  392.0 7.5 all-gather.2
  400.3 6.0 multiply_reduce_fusion.1.hin_ref
  406.3 292.2 %ssd_fwd_gate.1 = (bf16[4096,4096]{1,0:T(8,128)(2,1)}, bf16[4096,4096]{1,0:T(8,128)(2,1)}, f32[4096,4096]{1,0:T(8,128)}, f32[16,128,4096]{2,1,0:T(8,128)}, bf16[...) custom-call(bf16[4096,4352]{1,0:T(8,128)(2,1)} %conv_fwd.1.xc_ref, ...), custom_call_target="tpu_custom_call" | custom-call | flops 149999992832 | bytes 270000000 | tf_op jit(solution)/shard_map/ssd_fwd_gate/pallas_call | solution.py:350
  698.4 43.6 %fusion.10 = f32[4096,1024]{1,0:T(8,128)} fusion(bf16[4096,4096]{1,0:T(8,128)(2,1)} %get-tuple-element.60, bf16[4096,512]{1,0:T(8,128)(2,1)} %get-tuple-element.102, bf16[4096,512]{1,0:T(8,128)(2,1)} %get-tuple-element.101), kind=kOutput, calls=%fused_computation.27 | convolution fusion | flops 34376515584 | bytes 58720256 | tf_op jit(solution)/shard_map/dot_general | solution.py:29
  742.1 45.2 %fusion.5 = f32[4096,1024]{1,0:T(8,128)} fusion(bf16[4096,4096]{1,0:T(8,128)(2,1)} %get-tuple-element.59, bf16[4096,512]{1,0:T(8,128)(2,1)} %get-tuple-element.110, bf16[4096,512]{1,0:T(8,128)(2,1)} %get-tuple-element.111), kind=kOutput, calls=%fused_computation.16 | convolution fusion | flops 34376515584 | bytes 58720256 | tf_op jit(solution)/shard_map/dot_general | solution.py:29
  787.9 0.9 slice.153
  788.8 0.8 slice_reduce_fusion.3
  789.7 0.9 slice.152
  790.6 0.9 dynamic-slice_bitcast_fusion
  793.6 5.0 all-gather.8.cloned.1.call-done
  798.6 4.6 multiply_reduce_fusion.gin_ref
  803.3 1.5 copy-done.7
  804.8 2.1 multiply_reduce_fusion.2
  807.1 28.4 %slice_add_fusion.2 = f32[4096,512]{1,0:T(8,128)} fusion(f32[4096,1024]{1,0:T(8,128)} %collective-permute-done.2, bf16[4096,4096]{1,0:T(8,128)(2,1)} %get-tuple-element.60, bf16[4096,2048]{1,0:T(8,128)(2,1)} %param.10, s32[]{:T(128)S(6)} %select_n.110), kind=kOutput, calls=%fused_computation.12 | convolution fusion | flops 17181966336 | bytes 54525956 | tf_op jit(solution)/shard_map/dot_general | solution.py:29
  835.9 28.4 %slice_add_fusion.3 = f32[4096,512]{1,0:T(8,128)} fusion(f32[4096,1024]{1,0:T(8,128)} %collective-permute-done.1, bf16[4096,4096]{1,0:T(8,128)(2,1)} %get-tuple-element.59, bf16[4096,2048]{1,0:T(8,128)(2,1)} %param.11, s32[]{:T(128)S(6)} %select_n.110), kind=kOutput, calls=%fused_computation.13 | convolution fusion | flops 17181966336 | bytes 54525956 | tf_op jit(solution)/shard_map/dot_general | solution.py:29
  864.3 1.4 collective-permute-start.3
  866.3 256.3 %ssd_bwd.1 = (bf16[4096,4352]{1,0:T(8,128)(2,1)}, bf16[4096,64]{1,0:T(8,128)(2,1)}, f32[8,128]{1,0:T(8,128)}) custom-call(bf16[4096,4352]{1,0:T(8,128)(2,1)} %conv_fwd.1.xc_ref, f32[4096,128]{1,0:T(8,128)} %copy-done.4, bf16[4096,256]{1,0:T(8,128)(2,1)} %get-tuple-element.53.c3_ref, bf16[4096,256]{1,0:T(8,128)(2,1)} %get-tuple-element.62.d3_ref, ...), custom_call_target="tpu_custom_call" | custom-call | flops 149999992832 | bytes 220000000 | tf_op jit(solution)/shard_map/ssd_bwd/pallas_call | solution.py:471
  1122.7 1.0 multiply_multiply_fusion
  1123.7 1.3 collective-permute-start.4
  1125.7 28.2 %slice_add_fusion.4 = f32[4096,512]{1,0:T(8,128)} fusion(f32[4096,1024]{1,0:T(8,128)} %collective-permute-done.2, bf16[4096,4096]{1,0:T(8,128)(2,1)} %get-tuple-element.60, bf16[4096,2048]{1,0:T(8,128)(2,1)} %param.10, s32[]{:T(128)S(6)} %select_n.107), kind=kOutput, calls=%fused_computation.14 | convolution fusion | flops 17181966336 | bytes 54525956 | tf_op jit(solution)/shard_map/dot_general | solution.py:29
  1154.0 28.4 %slice_add_fusion.5 = f32[4096,512]{1,0:T(8,128)} fusion(f32[4096,1024]{1,0:T(8,128)} %collective-permute-done.1, bf16[4096,4096]{1,0:T(8,128)(2,1)} %get-tuple-element.59, bf16[4096,2048]{1,0:T(8,128)(2,1)} %param.11, s32[]{:T(128)S(6)} %select_n.107), kind=kOutput, calls=%fused_computation.15 | convolution fusion | flops 17181966336 | bytes 54525956 | tf_op jit(solution)/shard_map/dot_general | solution.py:29
  1182.4 15.8 collective-permute-done.3
  1198.2 9.2 add_convert_fusion.2
  1207.5 0.9 collective-permute-start.12
  1208.8 106.7 %conv_bwd.1 = (bf16[4096,4416]{1,0:T(8,128)(2,1)}, f32[32,4352]{1,0:T(8,128)S(1)}, f32[8,4352]{1,0:T(8,128)S(1)}, f32[16,4352]{1,0:T(8,128)S(1)}) custom-call(bf16[4096,4416]{1,0:T(8,128)(2,1)} %convolution_convert_fusion.x_ref, bf16[16,4416]{1,0:T(8,128)(2,1)} %collective-permute-done.halo_ref, bf16[4096,4352]{1,0:T(8,128)(2,1)} %get-tuple-element.70.d_ref, ...), custom_call_target="tpu_custom_call" | custom-call | flops 49999998976 | bytes 106954752 | tf_op jit(solution)/shard_map/conv_bwd/pallas_call | solution.py:164
  1316.1 0.8 fusion.17
  1316.8 1.1 constant_dynamic-update-slice_fusion.8
  1318.0 46.6 %fusion.9 = f32[4416,1024]{1,0:T(8,128)} fusion(bf16[4096,4416]{1,0:T(8,128)(2,1)} %constant_dynamic-update-slice_fusion.8, bf16[4096,512]{1,0:T(8,128)(2,1)} %get-tuple-element.102, bf16[4096,512]{1,0:T(8,128)(2,1)} %get-tuple-element.101), kind=kOutput, calls=%fused_computation.26 | convolution fusion | flops 37060870144 | bytes 62652416 | tf_op jit(solution)/shard_map/dot_general | solution.py:29
  1365.6 9.4 add_convert_fusion.3
  1375.0 1.7 collective-permute-start.8
  1376.7 87.5 %fusion = f32[4096,2048]{1,0:T(8,128)} fusion(bf16[4096,4416]{1,0:T(8,128)(2,1)} %constant_dynamic-update-slice_fusion.8, bf16[2048,8512]{0,1:T(8,128)(2,1)} %param.12), kind=kOutput, calls=%fused_computation.4 | convolution fusion | flops 74088185856 | bytes 88342528 | tf_op jit(solution)/shard_map/dot_general | solution.py:33
  1464.3 28.9 %slice_add_fusion.1 = f32[4416,512]{1,0:T(8,128)} fusion(f32[4416,1024]{1,0:T(8,128)} %collective-permute-done.6, bf16[4096,4416]{1,0:T(8,128)(2,1)} %constant_dynamic-update-slice_fusion.8, bf16[4096,2048]{1,0:T(8,128)(2,1)} %param.10, s32[]{:T(128)S(6)} %select_n.110), kind=kOutput, calls=%fused_computation.10 | convolution fusion | flops 18524307456 | bytes 58982404 | tf_op jit(solution)/shard_map/dot_general | solution.py:29
  1493.6 80.4 %add_convert_fusion = bf16[4096,2048]{1,0:T(8,128)(2,1)} fusion(f32[4096,2048]{1,0:T(8,128)} %fusion, bf16[4096,4096]{1,0:T(8,128)(2,1)} %get-tuple-element.60, bf16[2048,8512]{0,1:T(8,128)(2,1)} %param.12), kind=kOutput, calls=%fused_computation.1 | convolution fusion | flops 68736253952 | bytes 100663296 | tf_op jit(solution)/shard_map/dot_general | solution.py:33
  1574.5 29.0 %slice_add_fusion = f32[4416,512]{1,0:T(8,128)} fusion(f32[4416,1024]{1,0:T(8,128)} %collective-permute-done.6, bf16[4096,4416]{1,0:T(8,128)(2,1)} %constant_dynamic-update-slice_fusion.8, bf16[4096,2048]{1,0:T(8,128)(2,1)} %param.10, s32[]{:T(128)S(6)} %select_n.107), kind=kOutput, calls=%fused_computation.9 | convolution fusion | flops 18524307456 | bytes 58982404 | tf_op jit(solution)/shard_map/dot_general | solution.py:29
  1603.5 87.0 %collective-permute-done.7 = f32[4416,512]{1,0:T(8,128)} collective-permute-done((f32[4416,512]{1,0:T(8,128)}, f32[4416,512]{1,0:T(8,128)}, u32[]{:S(2)}, u32[]{:S(2)}) %collective-permute-start.7) | collective-permute-done | bytes 9044000 | tf_op jit(solution)/shard_map/ppermute | solution.py:593
  1690.5 9.8 add_convert_fusion.1
  1700.7 1.7 collective-permute-start.18
  1702.4 99.7 %collective-permute-done.18 = f32[26048]{0:T(1024)S(1)} collective-permute-done((f32[26048]{0:T(1024)S(1)}, f32[26048]{0:T(1024)S(1)}, u32[]{:S(2)}, u32[]{:S(2)}) %collective-permute-start.18) | collective-permute-done | bytes 104224 | tf_op jit(solution)/shard_map/ppermute | solution.py:591
  1804.7 4.5 constant_dynamic-update-slice_fusion.3
  1809.1 4.5 constant_dynamic-update-slice_fusion.7
  1813.6 4.5 constant_dynamic-update-slice_fusion.2
  1818.6 4.5 constant_dynamic-update-slice_fusion.6
  1823.1 4.6 constant_dynamic-update-slice_fusion.1
  1827.7 4.5 constant_dynamic-update-slice_fusion.5
  1832.2 4.5 constant_dynamic-update-slice_fusion
  1836.7 4.5 constant_dynamic-update-slice_fusion.4
  1841.2 2.4 constant_dynamic-update-slice_fusion.12
  1843.6 4.7 constant_dynamic-update-slice_fusion.11
  1848.3 2.4 constant_dynamic-update-slice_fusion.10
  1850.7 2.4 constant_dynamic-update-slice_fusion.9
  (137 shorter events, 15.8 us)
Async XLA Ops:
  7.2 393.1 %all-gather.6.cloned.1.call-start = ((), (), s32[]{:S(2)}) async-start(), calls=%async_computation | async-start | bytes 10485760 | tf_op jit(solution)/shard_map/all_gather | solution.py:533
  97.7 104.5 %collective-permute-start = (bf16[16,4416]{1,0:T(8,128)(2,1)}, bf16[16,4416]{1,0:T(8,128)(2,1)}, u32[]{:S(2)}, u32[]{:S(2)}) collective-permute-start(bf16[16,4416]{1,0:T(8,128)(2,1)} %slice.147), channel_id=1, source_target_pairs={{0,1},{1,2},{2,3},{4,5},{5,6},{6,7}} | collective-permute-start | bytes 423944 | tf_op jit(solution)/shard_map/ppermute | solution.py:527
  103.6 77.6 %copy-start.21 = (s32[4096]{0:T(1024)S(1)}, s32[4096]{0:T(1024)}, u32[]{:S(2)}) copy-start(s32[4096]{0:T(1024)} %add_select_fusion.1) | copy-start | bytes 49156
  103.6 77.6 %copy-start.23 = (s32[256]{0:T(256)S(1)}, s32[256]{0:T(256)}, u32[]{:S(2)}) copy-start(s32[256]{0:T(256)} %and_select_fusion) | copy-start | bytes 3076
  103.6 77.6 %copy-start.25 = (pred[256]{0:T(512)(128)(4,1)S(1)}, pred[256]{0:T(512)(128)(4,1)}, u32[]{:S(2)}) copy-start(pred[256]{0:T(512)(128)(4,1)} %iota_compare_fusion.1) | copy-start | bytes 772
  103.6 79.9 %copy-start.15 = (s32[8192]{0:T(1024)S(1)}, s32[8192]{0:T(1024)}, u32[]{:S(2)}) copy-start(s32[8192]{0:T(1024)} %add_select_fusion) | copy-start | bytes 98308
  187.2 13.6 copy-start.19
  187.2 13.6 copy-start.26
  187.2 15.0 copy-start.1
  200.7 43.2 %copy-start = (bf16[4096,64]{1,0:T(8,128)(2,1)}, bf16[4096,64]{1,0:T(8,128)(2,1)S(1)}, u32[]{:S(2)}) copy-start(bf16[4096,64]{1,0:T(8,128)(2,1)S(1)} %slice.148.dtr_ref) | copy-start | bytes 1572868
  202.2 41.7 %copy-start.2 = (f32[64]{0:T(128)S(1)}, f32[64]{0:T(128)}, u32[]{:S(2)}) copy-start(f32[64]{0:T(128)} %param.15) | copy-start | bytes 772
  202.2 41.7 %copy-start.3 = (f32[64]{0:T(128)S(1)}, f32[64]{0:T(128)}, u32[]{:S(2)}) copy-start(f32[64]{0:T(128)} %param.16) | copy-start | bytes 772
  310.6 1.3 copy-start.4
  311.9 1.4 copy-start.5
  313.3 485.3 %all-gather.8.cloned.1.call-start = ((), (), s32[]{:S(2)}) async-start(), calls=%async_computation.1 | async-start | bytes 10485760 | tf_op jit(solution)/shard_map/all_gather | solution.py:541
  313.8 85.8 %copy-start.28 = (pred[4,4]{0,1:T(4,128)(4,1)S(1)}, pred[4,4]{0,1:T(4,128)(4,1)}, u32[]{:S(2)}) copy-start(pred[4,4]{0,1:T(4,128)(4,1)} %iota_compare_fusion) | copy-start | bytes 52
  400.1 298.3 %copy-start.10 = (f32[4,4,4096]{2,0,1:T(4,128)}, f32[4,4,4096]{2,0,1:T(4,128)S(1)}, u32[]{:S(2)}) copy-start(f32[4,4,4096]{2,0,1:T(4,128)S(1)} %reshape.132) | copy-start | bytes 786436
  742.0 65.0 %collective-permute-start.2 = (f32[4096,1024]{1,0:T(8,128)}, f32[4096,1024]{1,0:T(8,128)}, u32[]{:S(2)}, u32[]{:S(2)}) collective-permute-start(f32[4096,1024]{1,0:T(8,128)} %fusion.10), channel_id=1, source_target_pairs={{0,1},{1,0},{2,3},{3,2},{4,5},{5,4},{6,7},{7,6}} | collective-permute-start | bytes 50331656 | tf_op jit(solution)/shard_map/ppermute | solution.py:560
  742.1 47.5 %copy-start.27 = (f32[64]{0:T(128)S(1)}, f32[64]{0:T(128)}, u32[]{:S(2)}) copy-start(f32[64]{0:T(128)} %get-tuple-element.108) | copy-start | bytes 772
  742.1 50.1 %copy-start.17 = (f32[8,4096]{1,0:T(8,128)S(1)}, f32[8,4096]{1,0:T(8,128)}, u32[]{:S(2)}) copy-start(f32[8,4096]{1,0:T(8,128)} %get-tuple-element.78) | copy-start | bytes 393220
  742.1 50.8 %copy-start.16 = (f32[8,4096]{1,0:T(8,128)S(1)}, f32[8,4096]{1,0:T(8,128)}, u32[]{:S(2)}) copy-start(f32[8,4096]{1,0:T(8,128)} %get-tuple-element.79) | copy-start | bytes 393220
  742.1 62.6 %copy-start.6 = (f32[128,4096]{1,0:T(8,128)S(1)}, f32[128,4096]{1,0:T(8,128)}, u32[]{:S(2)}) copy-start(f32[128,4096]{1,0:T(8,128)} %multiply_reduce_fusion.1.hin_ref) | copy-start | bytes 6291460
  787.3 48.6 %collective-permute-start.1 = (f32[4096,1024]{1,0:T(8,128)}, f32[4096,1024]{1,0:T(8,128)}, u32[]{:S(2)}, u32[]{:S(2)}) collective-permute-start(f32[4096,1024]{1,0:T(8,128)} %fusion.5), channel_id=1, source_target_pairs={{0,1},{1,0},{2,3},{3,2},{4,5},{5,4},{6,7},{7,6}} | collective-permute-start | bytes 50331656 | tf_op jit(solution)/shard_map/ppermute | solution.py:558
  803.3 1.5 copy-start.7
  835.5 362.7 %collective-permute-start.11 = (f32[4096,512]{1,0:T(8,128)}, f32[4096,512]{1,0:T(8,128)}, u32[]{:S(2)}, u32[]{:S(2)}) collective-permute-start(f32[4096,512]{1,0:T(8,128)} %slice_add_fusion.2), channel_id=1, source_target_pairs={{0,2},{1,3},{2,0},{3,1},{4,6},{5,7},{6,4},{7,5}} | collective-permute-start | bytes 25165832 | tf_op jit(solution)/shard_map/ppermute | solution.py:567
  864.3 333.9 %collective-permute-start.3 = (f32[4096,512]{1,0:T(8,128)}, f32[4096,512]{1,0:T(8,128)}, u32[]{:S(2)}, u32[]{:S(2)}) collective-permute-start(f32[4096,512]{1,0:T(8,128)} %slice_add_fusion.3), channel_id=1, source_target_pairs={{0,2},{1,3},{2,0},{3,1},{4,6},{5,7},{6,4},{7,5}} | collective-permute-start | bytes 25165832 | tf_op jit(solution)/shard_map/ppermute | solution.py:565
  866.3 256.3 %copy-start.8 = (f32[11,4352]{1,0:T(8,128)S(1)}, f32[11,4352]{1,0:T(8,128)}, u32[]{:S(2)}) copy-start(f32[11,4352]{1,0:T(8,128)} %maximum_convert_fusion) | copy-start | bytes 574468
  866.3 256.4 %copy-start.12 = (f32[4352]{0:T(1024)S(1)}, f32[4352]{0:T(1024)}, u32[]{:S(2)}) copy-start(f32[4352]{0:T(1024)} %get-tuple-element.98) | copy-start | bytes 52228
  866.3 256.4 %copy-start.13 = (f32[4352]{0:T(1024)S(1)}, f32[4352]{0:T(1024)}, u32[]{:S(2)}) copy-start(f32[4352]{0:T(1024)} %get-tuple-element.99) | copy-start | bytes 52228
  866.3 256.4 %copy-start.14 = (f32[4352]{0:T(1024)S(1)}, f32[4352]{0:T(1024)}, u32[]{:S(2)}) copy-start(f32[4352]{0:T(1024)} %get-tuple-element.100) | copy-start | bytes 52228
  866.3 256.4 %copy-start.18 = (f32[4352]{0:T(1024)S(1)}, f32[4352]{0:T(1024)}, u32[]{:S(2)}) copy-start(f32[4352]{0:T(1024)} %get-tuple-element.97) | copy-start | bytes 52228
  866.3 256.4 %copy-start.20 = (f32[4352]{0:T(1024)S(1)}, f32[4352]{0:T(1024)}, u32[]{:S(2)}) copy-start(f32[4352]{0:T(1024)} %param.14) | copy-start | bytes 52228
  1123.7 58.7 %collective-permute-start.4 = (f32[8,4352]{1,0:T(8,128)S(1)}, f32[8,4352]{1,0:T(8,128)S(1)}, u32[]{:S(2)}, u32[]{:S(2)}) collective-permute-start(f32[8,4352]{1,0:T(8,128)S(1)} %multiply_multiply_fusion), channel_id=1, source_target_pairs={{1,0},{2,1},{3,2},{5,4},{6,5},{7,6}} | collective-permute-start | bytes 417800 | tf_op jit(solution)/shard_map/ppermute | solution.py:574
  1207.5 366.5 %collective-permute-start.12 = (bf16[4096,512]{1,0:T(8,128)(2,1)}, bf16[4096,512]{1,0:T(8,128)(2,1)}, u32[]{:S(2)}, u32[]{:S(2)}) collective-permute-start(bf16[4096,512]{1,0:T(8,128)(2,1)} %add_convert_fusion.2), channel_id=1, source_target_pairs={{0,2},{1,3},{2,0},{3,1},{4,6},{5,7},{6,4},{7,5}} | collective-permute-start | bytes 12582920 | tf_op jit(solution)/shard_map/ppermute | solution.py:551
  1208.4 491.9 %collective-permute-start.13 = (bf16[4096,512]{1,0:T(8,128)(2,1)}, bf16[4096,512]{1,0:T(8,128)(2,1)}, u32[]{:S(2)}, u32[]{:S(2)}) collective-permute-start(bf16[4096,512]{1,0:T(8,128)(2,1)} %add_convert_fusion.2), channel_id=1, source_target_pairs={{0,1},{1,0},{2,3},{3,2},{4,5},{5,4},{6,7},{7,6}} | collective-permute-start | bytes 12582920 | tf_op jit(solution)/shard_map/ppermute | solution.py:552
  1208.7 107.0 %copy-start.22 = (f32[4096]{0:T(1024)S(1)}, f32[4096]{0:T(1024)}, u32[]{:S(2)}) copy-start(f32[4096]{0:T(1024)} %reduce_sum.99) | copy-start | bytes 49156
  1208.7 107.0 %copy-start.24 = (f32[64]{0:T(128)S(1)}, f32[64]{0:T(128)}, u32[]{:S(2)}) copy-start(f32[64]{0:T(128)} %reduce_sum.98) | copy-start | bytes 772
  1208.7 108.1 %copy-start.9 = (bf16[4096,64]{1,0:T(8,128)(2,1)S(1)}, bf16[4096,64]{1,0:T(8,128)(2,1)}, u32[]{:S(2)}) copy-start(bf16[4096,64]{1,0:T(8,128)(2,1)} %get-tuple-element.74) | copy-start | bytes 1572868
  1315.8 48.8 %collective-permute-start.5 = (f32[26048]{0:T(1024)S(1)}, f32[26048]{0:T(1024)S(1)}, u32[]{:S(2)}, u32[]{:S(2)}) collective-permute-start(f32[26048]{0:T(1024)S(1)} %concatenate.19), channel_id=1, source_target_pairs={{0,1},{1,0},{2,3},{3,2},{4,5},{5,4},{6,7},{7,6}} | collective-permute-start | bytes 312584 | tf_op jit(solution)/shard_map/ppermute | solution.py:586
  1365.3 99.0 %collective-permute-start.6 = (f32[4416,1024]{1,0:T(8,128)}, f32[4416,1024]{1,0:T(8,128)}, u32[]{:S(2)}, u32[]{:S(2)}) collective-permute-start(f32[4416,1024]{1,0:T(8,128)} %fusion.9), channel_id=1, source_target_pairs={{0,1},{1,0},{2,3},{3,2},{4,5},{5,4},{6,7},{7,6}} | collective-permute-start | bytes 54263816 | tf_op jit(solution)/shard_map/ppermute | solution.py:590
  1375.0 199.2 %collective-permute-start.8 = (bf16[4096,512]{1,0:T(8,128)(2,1)}, bf16[4096,512]{1,0:T(8,128)(2,1)}, u32[]{:S(2)}, u32[]{:S(2)}) collective-permute-start(bf16[4096,512]{1,0:T(8,128)(2,1)} %add_convert_fusion.3), channel_id=1, source_target_pairs={{0,2},{1,3},{2,0},{3,1},{4,6},{5,7},{6,4},{7,5}} | collective-permute-start | bytes 12582920 | tf_op jit(solution)/shard_map/ppermute | solution.py:551
  1376.7 323.6 %collective-permute-start.9 = (bf16[4096,512]{1,0:T(8,128)(2,1)}, bf16[4096,512]{1,0:T(8,128)(2,1)}, u32[]{:S(2)}, u32[]{:S(2)}) collective-permute-start(bf16[4096,512]{1,0:T(8,128)(2,1)} %add_convert_fusion.3), channel_id=1, source_target_pairs={{0,1},{1,0},{2,3},{3,2},{4,5},{5,4},{6,7},{7,6}} | collective-permute-start | bytes 12582920 | tf_op jit(solution)/shard_map/ppermute | solution.py:552
  1493.1 197.3 %collective-permute-start.7 = (f32[4416,512]{1,0:T(8,128)}, f32[4416,512]{1,0:T(8,128)}, u32[]{:S(2)}, u32[]{:S(2)}) collective-permute-start(f32[4416,512]{1,0:T(8,128)} %slice_add_fusion.1), channel_id=1, source_target_pairs={{0,2},{1,3},{2,0},{3,1},{4,6},{5,7},{6,4},{7,5}} | collective-permute-start | bytes 27131912 | tf_op jit(solution)/shard_map/ppermute | solution.py:593
  1574.0 126.3 %collective-permute-start.14 = (bf16[4096,512]{1,0:T(8,128)(2,1)}, bf16[4096,512]{1,0:T(8,128)(2,1)}, u32[]{:S(2)}, u32[]{:S(2)}) collective-permute-start(bf16[4096,512]{1,0:T(8,128)(2,1)} %collective-permute-done.12), channel_id=1, source_target_pairs={{0,1},{1,0},{2,3},{3,2},{4,5},{5,4},{6,7},{7,6}} | collective-permute-start | bytes 12582920 | tf_op jit(solution)/shard_map/ppermute | solution.py:553
  1574.2 126.1 %collective-permute-start.10 = (bf16[4096,512]{1,0:T(8,128)(2,1)}, bf16[4096,512]{1,0:T(8,128)(2,1)}, u32[]{:S(2)}, u32[]{:S(2)}) collective-permute-start(bf16[4096,512]{1,0:T(8,128)(2,1)} %collective-permute-done.8), channel_id=1, source_target_pairs={{0,1},{1,0},{2,3},{3,2},{4,5},{5,4},{6,7},{7,6}} | collective-permute-start | bytes 12582920 | tf_op jit(solution)/shard_map/ppermute | solution.py:553
  1603.5 97.2 %copy-start.11 = (f32[26048]{0:T(1024)S(1)}, f32[26048]{0:T(1024)}, u32[]{:S(2)}) copy-start(f32[26048]{0:T(1024)} %add.197) | copy-start | bytes 312580
  1700.3 117.8 %collective-permute-start.15 = (bf16[4416,512]{1,0:T(8,128)(2,1)}, bf16[4416,512]{1,0:T(8,128)(2,1)}, u32[]{:S(2)}, u32[]{:S(2)}) collective-permute-start(bf16[4416,512]{1,0:T(8,128)(2,1)} %add_convert_fusion.1), channel_id=1, source_target_pairs={{0,2},{1,3},{2,0},{3,1},{4,6},{5,7},{6,4},{7,5}} | collective-permute-start | bytes 13565960 | tf_op jit(solution)/shard_map/ppermute | solution.py:551
  1700.7 101.4 %collective-permute-start.18 = (f32[26048]{0:T(1024)S(1)}, f32[26048]{0:T(1024)S(1)}, u32[]{:S(2)}, u32[]{:S(2)}) collective-permute-start(f32[26048]{0:T(1024)S(1)} %copy-done.11), channel_id=1, source_target_pairs={{0,2},{1,3},{2,0},{3,1},{4,6},{5,7},{6,4},{7,5}} | collective-permute-start | bytes 312584 | tf_op jit(solution)/shard_map/ppermute | solution.py:591
  1804.7 43.6 %collective-permute-start.16 = (bf16[4416,512]{1,0:T(8,128)(2,1)}, bf16[4416,512]{1,0:T(8,128)(2,1)S(1)}, u32[]{:S(2)}, u32[]{:S(2)}) collective-permute-start(bf16[4416,512]{1,0:T(8,128)(2,1)} %add_convert_fusion.1), channel_id=1, source_target_pairs={{0,1},{1,0},{2,3},{3,2},{4,5},{5,4},{6,7},{7,6}} | collective-permute-start | bytes 13565960 | tf_op jit(solution)/shard_map/ppermute | solution.py:552
  1818.1 32.6 %collective-permute-start.17 = (bf16[4416,512]{1,0:T(8,128)(2,1)}, bf16[4416,512]{1,0:T(8,128)(2,1)S(1)}, u32[]{:S(2)}, u32[]{:S(2)}) collective-permute-start(bf16[4416,512]{1,0:T(8,128)(2,1)} %collective-permute-done.15), channel_id=1, source_target_pairs={{0,1},{1,0},{2,3},{3,2},{4,5},{5,4},{6,7},{7,6}} | collective-permute-start | bytes 13565960 | tf_op jit(solution)/shard_map/ppermute | solution.py:553
  1823.1 18.1 slice-start
  1832.2 9.0 slice-start.1
Sparse Core Ops, SparseCore 0:
  313.5 57.1 all-gather.5
  742.2 56.3 all-gather.7
